TPU v7x, 32 devices: a whole 2x2x4 slice. The times are simulated.
32 devices in a mesh: rng: 2 (over x), az: 16 (over z, y, core).
Axes of the slice: x: 2, y: 2, z: 4, core: 2. Of those that a mesh axis runs over, the one named last changes fastest.
Arguments:
- spectrum: float32 [1024, 2, 32768], P('rng', None, 'az'), may hold values from -9 to 9
- src_block: int32 [256, 8], P('az', 'rng'), may hold values from 0 to 6, as said below
- offsets: int32 [256, 1024], P('az', 'rng'), may hold values from 0 to 127
- tap_weights: float32 [8, 256, 1024], P(None, 'az', 'rng'), may hold values from -2 to 2
Outputs:
- image: float32 [1024, 2, 32768], P(('rng', 'az'))
Inputs may be any that keep to these rules, and one draw needn't show every extreme that they name: src_block[g, b] lies between min(b, 6) and min(b + 5, 6); a shift of 5 blocks occurs in every draw.
All inputs are finite; a program needn't handle non-finite values.
Results may differ from a plain program's by a relative error of at most 0.00007.
Values sent between devices are 32-bit elements; how exact they have to be, the bound alone decides.
A program may use at most 192 MiB of HBM per device.

v0:
```python
import functools
import math

import jax
import jax.numpy as jnp
import numpy as np
from jax import lax
from jax.experimental import pallas as pl
from jax.experimental.pallas import tpu as pltpu
from jax.sharding import PartitionSpec as P

BLOCK = 128
GW = 128
TAPS = 8
SHIFT_B = 5
WINDOW = 144
CHUNK_GROUPS = 2

MESH = pl.DeviceIdType.MESH


def split_np(x):
    hi = x.astype(jnp.bfloat16)
    lo = (x - hi.astype(np.float64)).astype(jnp.bfloat16)
    return hi, lo


def split(x):
    hi = x.astype(jnp.bfloat16)
    lo = (x - hi.astype(jnp.float32)).astype(jnp.bfloat16)
    return hi, lo


def dft_tables(az_count, groups, per_chunk):
    total_groups = az_count * groups
    chunks = groups // per_chunk
    total_len = total_groups * GW
    k1 = np.arange(total_groups)
    ch, az, gl = np.meshgrid(np.arange(chunks), np.arange(az_count), np.arange(per_chunk), indexing="ij")
    g = (az * groups + ch * per_chunk + gl).reshape(-1)
    angle = 2.0 * np.pi * ((k1[:, None] * g[None, :]) % total_groups) / total_groups
    first = np.empty((2, total_groups, g.size, 2))
    first[0, :, :, 0] = np.cos(angle)
    first[0, :, :, 1] = -np.sin(angle)
    first[1, :, :, 0] = np.sin(angle)
    first[1, :, :, 1] = np.cos(angle)
    first = first.reshape(2 * total_groups, 2 * total_groups)
    l = np.arange(GW)
    turn = 2.0 * np.pi * (k1[:, None] * l[None, :]) / total_len
    twist = np.stack([np.cos(turn), np.sin(turn)]).astype(np.float32) / np.float32(total_len)
    inner = 2.0 * np.pi * ((l[:, None] * l[None, :]) % GW) / GW
    second = np.empty((2, GW, 2, GW))
    second[0, :, 0] = np.cos(inner)
    second[0, :, 1] = -np.sin(inner)
    second[1, :, 0] = np.sin(inner)
    second[1, :, 1] = np.cos(inner)
    second = second.reshape(2 * GW, 2 * GW)
    a_hi, a_lo = split_np(first)
    b_hi, b_lo = split_np(second)
    return a_hi, a_lo, twist, b_hi, b_lo


def remap_group(ext, out, sub, gl, blocks, src_of, off_row, weight_row):
    energy = jnp.zeros((8, GW), jnp.float32)
    for b in range(blocks):
        start = src_of(b) * (BLOCK * sub) + 2 * gl
        source = jnp.concatenate(
            [ext[pl.ds(start + c, WINDOW, stride=sub), :] for c in range(2)], axis=1
        )
        at = lax.broadcasted_iota(jnp.int32, (WINDOW, BLOCK), 0) - off_row(b)
        taps = jnp.zeros((WINDOW, BLOCK), jnp.float32)
        for t in range(TAPS):
            taps = jnp.where(at == t, weight_row(t, b), taps)
        t_hi, t_lo = split(taps)
        s_hi, s_lo = split(source)
        left = jnp.concatenate([t_hi, t_lo, t_hi], axis=0)
        right = jnp.concatenate([s_hi, s_hi, s_lo], axis=0)
        value = lax.dot_general(
            left, right, (((0,), (0,)), ((), ())), preferred_element_type=jnp.float32
        )
        for c in range(2):
            half = value[:, c * GW:(c + 1) * GW]
            out[pl.ds(b * BLOCK * sub + 2 * gl + c, BLOCK, stride=sub), :] = half
            energy = energy + jnp.sum((half * half).reshape(BLOCK // 8, 8, GW), axis=0)
    return energy


def exchange_kernel(rows, blocks, chunks, per_chunk, counts, src_ref, off_ref, w_ref, spec_ref,
                    recv_ref, energy_ref, *scratch):
    ext, stage = scratch[:chunks], scratch[chunks:2 * chunks]
    (e_own, e_rng, e_sum, e_az, local_sem, halo_send, halo_recv,
     part_send, part_recv, e_send, e_recv) = scratch[2 * chunks:]
    rng_count, az_count = lax.axis_size("rng"), lax.axis_size("az")
    p, q = lax.axis_index("rng"), lax.axis_index("az")
    sub = 2 * per_chunk
    piece = rows // az_count
    half = max(az_count // 2, 1)
    side, place = q // half, q % half

    def local(c):
        return pltpu.make_async_copy(
            spec_ref.at[:, c], ext[c].at[pl.ds(0, rows)], local_sem.at[c])

    def halo(c, i):
        return pltpu.make_async_remote_copy(
            src_ref=spec_ref.at[pl.ds(0, counts[i]), c],
            dst_ref=ext[c].at[pl.ds(rows + sum(counts[:i]), counts[i])],
            send_sem=halo_send.at[c, i], recv_sem=halo_recv.at[c, i],
            device_id={"rng": (p + rng_count - i - 1) % rng_count}, device_id_type=MESH)

    reach = [i for i in range(len(counts)) if i + 1 < rng_count]
    for c in range(chunks):
        for i in reach:
            pl.when(p >= i + 1)(lambda c=c, i=i: halo(c, i).start())
        local(c).start()

    energy = jnp.zeros((8, GW), jnp.float32)
    for c in range(chunks):
        local(c).wait()
        for i in reach:
            pl.when(p + i + 1 < rng_count)(lambda c=c, i=i: halo(c, i).wait_recv())
        flat = ext[c].reshape(ext[c].shape[0] * sub, GW)
        out = stage[c].reshape(rows * sub, GW)
        for gl in range(per_chunk):
            g = c * per_chunk + gl
            energy = energy + remap_group(
                flat, out, sub, gl, blocks,
                lambda b: src_ref[g, b],
                lambda b: off_ref[pl.ds(g, 1), pl.ds(b * BLOCK, BLOCK)],
                lambda t, b: w_ref[t, pl.ds(g, 1), pl.ds(b * BLOCK, BLOCK)],
            )

        def send(peer, c=c):
            pltpu.make_async_remote_copy(
                src_ref=stage[c].at[pl.ds(peer * piece, piece)],
                dst_ref=recv_ref.at[c, q],
                send_sem=part_send.at[c], recv_sem=part_recv.at[c],
                device_id={"az": peer}, device_id_type=MESH).start()

        @pl.loop(0, half)
        def _(j):
            send((1 - side) * half + (place + j) % half)

        @pl.loop(1, half)
        def _(j):
            send(side * half + (place + j) % half)

        pltpu.make_async_copy(
            stage[c].at[pl.ds(q * piece, piece)], recv_ref.at[c, q], part_recv.at[c]).start()

    def share(src, dst, slot, axis, peer, stage_at):
        return pltpu.make_async_remote_copy(
            src_ref=src, dst_ref=dst.at[slot], send_sem=e_send.at[stage_at],
            recv_sem=e_recv.at[stage_at], device_id={axis: peer}, device_id_type=MESH)

    def spread(src, dst, slot, axis, count, stage_at):
        @pl.loop(1, count)
        def _(j):
            share(src, dst, slot, axis, (slot + j) % count, stage_at).start()
        others = dst.at[pl.ds(0, count - 1)]
        pltpu.make_async_copy(others, others, e_send.at[stage_at]).wait()
        pltpu.make_async_copy(others, others, e_recv.at[stage_at]).wait()

    e_own[...] = energy
    e_rng[p] = energy
    spread(e_own, e_rng, p, "rng", rng_count, 0)
    energy = jnp.sum(e_rng[...], axis=0)
    e_sum[...] = energy
    e_az[q] = energy
    spread(e_sum, e_az, q, "az", az_count, 1)
    energy_ref[...] = jnp.sum(e_az[...], axis=0)

    for c in range(chunks):
        pltpu.make_async_copy(recv_ref.at[c], recv_ref.at[c], part_recv.at[c]).wait()
        sent = stage[c].at[pl.ds(0, rows - piece)]
        pltpu.make_async_copy(sent, sent, part_send.at[c]).wait()
        for i in reach:
            pl.when(p >= i + 1)(lambda c=c, i=i: halo(c, i).wait_send())


def exchange(spec, local_src, offsets, weights, counts, per_chunk, rng_count, az_count):
    rows, chunks, sub, _ = spec.shape
    blocks = rows // BLOCK
    piece = rows // az_count
    vmem = pl.BlockSpec(memory_space=pltpu.VMEM)
    hbm = pl.BlockSpec(memory_space=pl.ANY)
    tile = (8, GW)
    dma = pltpu.SemaphoreType.DMA
    return pl.pallas_call(
        functools.partial(exchange_kernel, rows, blocks, chunks, per_chunk, counts),
        out_shape=(
            jax.ShapeDtypeStruct((chunks, az_count, piece, sub, GW), jnp.float32),
            jax.ShapeDtypeStruct(tile, jnp.float32),
        ),
        in_specs=[pl.BlockSpec(memory_space=pltpu.SMEM), vmem, vmem, hbm],
        out_specs=(hbm, vmem),
        scratch_shapes=[pltpu.VMEM((rows + sum(counts), sub, GW), jnp.float32)] * chunks
        + [pltpu.VMEM((rows, sub, GW), jnp.float32)] * chunks
        + [
            pltpu.VMEM(tile, jnp.float32),
            pltpu.VMEM((rng_count,) + tile, jnp.float32),
            pltpu.VMEM(tile, jnp.float32),
            pltpu.VMEM((az_count,) + tile, jnp.float32),
            dma((chunks,)),
            dma((chunks, len(counts))),
            dma((chunks, len(counts))),
            dma((chunks,)),
            dma((chunks,)),
            dma((2,)),
            dma((2,)),
        ],
        compiler_params=pltpu.CompilerParams(has_side_effects=True, vmem_limit_bytes=60 * 1024 * 1024),
    )(local_src, offsets, weights, spec)


def dft_kernel(rows, chunks, scale_ref, a_hi_ref, a_lo_ref, twist_ref, b_hi_ref, b_lo_ref, *rest):
    parts_ref, out_ref = rest
    total_groups = a_hi_ref.shape[0] // 2
    scale = scale_ref[0, 0]
    halves = total_groups // GW
    pair = min(2, rows)
    wide = pair * GW
    for first in range(0, rows, pair):
        x = jnp.concatenate([
            jnp.concatenate(
                [parts_ref[c, :, r].reshape(2 * total_groups // chunks, GW) for c in range(chunks)], axis=0)
            for r in range(first, first + pair)], axis=1)
        x_hi, x_lo = split(x)
        both = jnp.dot(a_hi_ref[...], jnp.concatenate([x_hi, x_lo], axis=1), preferred_element_type=jnp.float32)
        y = both[:, :wide] + both[:, wide:] + jnp.dot(a_lo_ref[...], x_hi, preferred_element_type=jnp.float32)
        t_re, t_im = twist_ref[0], twist_ref[1]
        turned = []
        for i in range(pair):
            y_re = y[:total_groups, i * GW:(i + 1) * GW]
            y_im = y[total_groups:, i * GW:(i + 1) * GW]
            turned.append(jnp.concatenate([y_re * t_re - y_im * t_im, y_re * t_im + y_im * t_re], axis=1))
        z_hi, z_lo = split(jnp.concatenate(turned, axis=0) * scale)
        nt = (((1,), (1,)), ((), ()))
        v = (
            lax.dot_general(b_hi_ref[...], z_hi, nt, preferred_element_type=jnp.float32)
            + lax.dot_general(b_hi_ref[...], z_lo, nt, preferred_element_type=jnp.float32)
            + lax.dot_general(b_lo_ref[...], z_hi, nt, preferred_element_type=jnp.float32)
        )
        for i in range(pair):
            for c in range(2):
                for h in range(halves):
                    out_ref[first + i, pl.ds(2 * h + c, GW, stride=2 * halves), :] = (
                        v[c * GW:(c + 1) * GW, i * total_groups + h * GW:i * total_groups + (h + 1) * GW])


def inverse(parts, scale, tables):
    a_hi, a_lo, twist, b_hi, b_lo = tables
    chunks, az, rows, sub, _ = parts.shape
    step = min(rows, 4)
    whole = lambda shape: pl.BlockSpec(shape, lambda i: (0,) * len(shape))
    return pl.pallas_call(
        functools.partial(dft_kernel, step, chunks),
        out_shape=jax.ShapeDtypeStruct((rows, a_hi.shape[0], GW), jnp.float32),
        grid=(rows // step,),
        in_specs=[pl.BlockSpec(memory_space=pltpu.SMEM)]
        + [whole(t.shape) for t in tables]
        + [pl.BlockSpec((chunks, az, step, sub, GW), lambda i: (0, 0, i, 0, 0))],
        out_specs=pl.BlockSpec((step, a_hi.shape[0], GW), lambda i: (i, 0, 0)),
        cost_estimate=pl.CostEstimate(flops=10_000_000_000, bytes_accessed=20_000_000, transcendentals=0),
    )(scale, *tables, parts)


def halo_counts(rows_dev, rng_count):
    total = rows_dev * rng_count
    halo = min(rows_dev - BLOCK + SHIFT_B * BLOCK, total - 2 * BLOCK) + WINDOW - rows_dev
    counts = []
    distance = 1
    while halo > 0:
        counts.append(min(halo, rows_dev))
        halo -= rows_dev
        distance += 1
    return counts


def body(spectrum, src_block, offsets, tap_weights):
    rows_dev = spectrum.shape[0]
    columns = spectrum.shape[2]
    groups = columns // GW
    blocks_dev = rows_dev // BLOCK
    rng_count = lax.axis_size("rng")
    az_count = lax.axis_size("az")
    rows_after = rows_dev // az_count
    per_chunk = min(CHUNK_GROUPS, groups)
    total_len = columns * az_count
    total_cells = rows_dev * rng_count * total_len
    tables = dft_tables(az_count, groups, per_chunk)
    spec = spectrum.reshape(rows_dev, 2, groups, GW).transpose(0, 2, 1, 3).reshape(rows_dev, groups // per_chunk, 2 * per_chunk, GW)
    local_src = src_block - lax.axis_index("rng") * blocks_dev
    counts = halo_counts(rows_dev, rng_count)
    parts, energies = exchange(
        spec, local_src, offsets, tap_weights, counts, per_chunk, rng_count, az_count)
    energy = jnp.sum(energies) / total_len
    scale = lax.rsqrt(energy / total_cells + 1e-06).reshape(1, 1)
    image = inverse(parts, scale, tables)
    return (
        image.reshape(rows_after, total_len // GW, 2, GW)
        .transpose(0, 2, 1, 3)
        .reshape(rows_after, 2, total_len)
    )


def solution(mesh):
    placed = (P("rng", None, "az"), P("az", "rng"), P("az", "rng"), P(None, "az", "rng"))
    return jax.shard_map(
        body, mesh=mesh, in_specs=placed, out_specs=P(("rng", "az"), None, None), check_vma=False
    )
```

profile of v0, /device:TPU:0, one launch (start us, length us, event | category | flops | bytes accessed | tf_op | source)
XLA Modules:
  0.0 244.6 jit_solution(13739318049464844604)
XLA Ops:
  0.0 0.8 copy.13
  0.8 0.6 broadcast_subtract_fusion.src_ref
  1.4 215.4 %shard_map.91 = (f32[8,16,32,4,128]{4,3,2,1,0:T(4,128)}, f32[8,128]{1,0:T(8,128)}) custom-call(s32[16,4]{1,0:T(8,128)} %broadcast_subtract_fusion.src_ref, s32[16,512]{1,0:T(8,128)} %off_ref.1, f32[8,16,512]{2,1,0:T(8,128)} %w_ref.1, f32[512,8,4,128]{3,2,1,0:T(4,128)} %bitcast.11), custom_call_target="tpu_custom_call" | custom-call | tf_op jit(solution)/shard_map/pallas_call | solution.py:189
  216.7 1.3 reduce_sum.9
  218.7 25.9 %shard_map.92 = f32[32,512,128]{2,1,0:T(8,128)} custom-call(f32[1,1]{1,0:T(1,128)} %bitcast.3.scale_ref, bf16[512,512]{1,0:T(8,128)(2,1)} %constant.28.clone.a_hi_ref, bf16[512,512]{1,0:T(8,128)(2,1)} %constant.29.clone.a_lo_ref, f32[2,256,128]{2,1,0:T(8,128)} %constant.30.clone.twist_ref, bf16[256,256]{1,0:T(8,128)(2,1)} %constant.31.clone.b_hi_ref, ...), custom_call_target="tpu_custom_call" | custom-call | flops 10000000000 | bytes 20000000 | tf_op jit(solution)/shard_map/pallas_call | solution.py:256
where the time goes:
time: 245 us
  Pallas kernels  241 us (98%)
    pallas_call x1, Pallas kernels, exchange(): pl.pallas_call(functools.partial(exchange_kernel, rows, blocks, chunks, p...  215 us
    pallas_call x1, Pallas kernels, inverse(): pl.pallas_call(functools.partial(dft_kernel, step, chunks), out_shape=jax...  25.9 us

commit v1 on v0

v1 whole, which is shorter than its diff:
```python
import functools

import jax
import jax.numpy as jnp
import numpy as np
from jax import lax
from jax.experimental import pallas as pl
from jax.experimental.pallas import tpu as pltpu
from jax.sharding import PartitionSpec as P

BLOCK = 128
GW = 128
TAPS = 8
SHIFT_B = 5
WINDOW = 144
LAG = 2
STEP = 4

MESH = pl.DeviceIdType.MESH


def split_np(x):
    hi = x.astype(jnp.bfloat16)
    lo = (x - hi.astype(np.float64)).astype(jnp.bfloat16)
    return hi, lo


def split(x):
    hi = x.astype(jnp.bfloat16)
    lo = (x - hi.astype(jnp.float32)).astype(jnp.bfloat16)
    return hi, lo


def plan(groups):
    last = max(1, groups // 4)
    single = min(groups - last, (3 * groups) // 8)
    sizes = [1] * single
    left = groups - last - single
    sizes += [2] * (left // 2) + [1] * (left % 2) + [last]
    starts = [sum(sizes[:i]) for i in range(len(sizes))]
    return tuple(zip(starts, sizes))


def dft_tables(az_count, groups, chunks):
    total_groups = az_count * groups
    total_len = total_groups * GW
    k1 = np.arange(total_groups)
    stage_one = []
    for start, per in chunks:
        gl, az = np.meshgrid(np.arange(start, start + per), np.arange(az_count), indexing="ij")
        g = az * groups + gl
        angle = 2.0 * np.pi * ((k1[:, None, None] * g[None]) % total_groups) / total_groups
        first = np.empty((2, total_groups, per, 2, az_count))
        first[0, :, :, 0] = np.cos(angle)
        first[0, :, :, 1] = -np.sin(angle)
        first[1, :, :, 0] = np.sin(angle)
        first[1, :, :, 1] = np.cos(angle)
        hi, lo = split_np(first.reshape(2 * total_groups, 2 * per * az_count))
        stage_one.append(np.concatenate([hi, hi, lo], axis=1))
    l = np.arange(GW)
    turn = 2.0 * np.pi * (k1[:, None] * l[None, :]) / total_len
    twist = np.stack([np.cos(turn), np.sin(turn)]).astype(np.float32) / np.float32(total_len)
    inner = 2.0 * np.pi * ((l[:, None] * l[None, :]) % GW) / GW
    second = np.empty((2, GW, 2, GW))
    second[0, :, 0] = np.cos(inner)
    second[0, :, 1] = -np.sin(inner)
    second[1, :, 0] = np.sin(inner)
    second[1, :, 1] = np.cos(inner)
    b_hi, b_lo = split_np(second.reshape(2 * GW, 2 * GW))
    return stage_one + [twist, b_hi, b_lo]


def remap_group(ext, out, sub, gl, blocks, src_of, off_row, weight_row):
    energy = jnp.zeros((8, GW), jnp.float32)
    for b in range(blocks):
        start = src_of(b) * (BLOCK * 2)
        source = jnp.concatenate(
            [ext[pl.ds(start + c, WINDOW, stride=2), :] for c in range(2)], axis=1
        )
        at = lax.broadcasted_iota(jnp.int32, (WINDOW, BLOCK), 0) - off_row(b)
        taps = jnp.zeros((WINDOW, BLOCK), jnp.float32)
        for t in range(TAPS):
            taps = jnp.where(at == t, weight_row(t, b), taps)
        t_hi, t_lo = split(taps)
        s_hi, s_lo = split(source)
        left = jnp.concatenate([t_hi, t_lo, t_hi], axis=0)
        right = jnp.concatenate([s_hi, s_hi, s_lo], axis=0)
        value = lax.dot_general(
            left, right, (((0,), (0,)), ((), ())), preferred_element_type=jnp.float32
        )
        for c in range(2):
            half = value[:, c * GW:(c + 1) * GW]
            out[pl.ds(b * BLOCK * sub + 2 * gl + c, BLOCK, stride=sub), :] = half
            energy = energy + jnp.sum((half * half).reshape(BLOCK // 8, 8, GW), axis=0)
    return energy


def fused_kernel(rows, blocks, groups, chunks, counts, step, cells, src_ref, off_hbm, w_hbm, spec_ref, *rest):
    n = len(chunks)
    tables_hbm, image_ref, scratch = rest[:n + 3], rest[n + 3], rest[n + 4:]
    ext, scratch = scratch[:groups], scratch[groups:]
    stage, scratch = scratch[:n], scratch[n:]
    recv, scratch = scratch[:n], scratch[n:]
    tables, scratch = scratch[:n + 3], scratch[n + 3:]
    (y_acc, off_ref, w_ref, e_own, e_az, e_sum, e_rng, small_sem, table_sem, local_sem, halo_send, halo_recv,
     part_send, part_recv, last_recv, e_send, e_recv) = scratch
    a_refs, (twist_ref, b_hi_ref, b_lo_ref) = tables[:n], tables[n:]
    rng_count, az_count = lax.axis_size("rng"), lax.axis_size("az")
    p, q = lax.axis_index("rng"), lax.axis_index("az")
    piece = rows // az_count
    half = max(az_count // 2, 1)
    side, place = q // half, q % half
    subsets = piece // step
    total_groups = az_count * groups
    wide = 2 * GW

    def local(g):
        return pltpu.make_async_copy(
            spec_ref.at[:, g], ext[g].at[pl.ds(0, rows)], local_sem.at[g])

    def halo(g, i):
        return pltpu.make_async_remote_copy(
            src_ref=spec_ref.at[pl.ds(0, counts[i]), g],
            dst_ref=ext[g].at[pl.ds(rows + sum(counts[:i]), counts[i])],
            send_sem=halo_send.at[g, i], recv_sem=halo_recv.at[g, i],
            device_id={"rng": (p + rng_count - i - 1) % rng_count}, device_id_type=MESH)

    def table(i):
        return pltpu.make_async_copy(tables_hbm[i], tables[i], table_sem.at[i])

    small = [pltpu.make_async_copy(off_hbm, off_ref, small_sem.at[0]),
             pltpu.make_async_copy(w_hbm, w_ref, small_sem.at[1])]
    for copy in small:
        copy.start()
    local(0).start()

    barrier = pltpu.get_barrier_semaphore()

    @pl.loop(1, rng_count)
    def _(j):
        pl.semaphore_signal(barrier, inc=1, device_id={"rng": (p + j) % rng_count}, device_id_type=MESH)

    @pl.loop(1, az_count)
    def _(j):
        pl.semaphore_signal(barrier, inc=1, device_id={"az": (q + j) % az_count}, device_id_type=MESH)

    for g in range(1, groups):
        local(g).start()
    for i in range(n + 3):
        table(i).start()
    pl.semaphore_wait(barrier, rng_count + az_count - 2)

    reach = [i for i in range(len(counts)) if i + 1 < rng_count]
    for g in range(groups):
        for i in reach:
            pl.when(p >= i + 1)(lambda g=g, i=i: halo(g, i).start())
    for copy in small:
        copy.wait()

    def remap(c):
        start, per = chunks[c]
        sub = 2 * per
        out = stage[c].reshape(rows * sub, GW)
        energy = jnp.zeros((8, GW), jnp.float32)
        for gl in range(per):
            g = start + gl
            local(g).wait()
            for i in reach:
                pl.when(p + i + 1 < rng_count)(lambda g=g, i=i: halo(g, i).wait_recv())
            energy = energy + remap_group(
                ext[g].reshape(ext[g].shape[0] * 2, GW), out, sub, gl, blocks,
                lambda b: jnp.maximum(src_ref[b, g] - p * blocks, 0),
                lambda b: off_ref[pl.ds(g, 1), pl.ds(b * BLOCK, BLOCK)],
                lambda t, b: w_ref[t, pl.ds(g, 1), pl.ds(b * BLOCK, BLOCK)],
            )
        recv[c][q] = stage[c][pl.ds(q * piece, piece)]
        return energy

    def spread(send):
        @pl.loop(0, half)
        def _(j):
            send((1 - side) * half + (place + j) % half)

        @pl.loop(1, half)
        def _(j):
            send(side * half + (place + j) % half)

    def send_chunk(c):
        spread(lambda peer: pltpu.make_async_remote_copy(
            src_ref=stage[c].at[pl.ds(peer * piece, piece)],
            dst_ref=recv[c].at[q],
            send_sem=part_send.at[c], recv_sem=part_recv.at[c],
            device_id={"az": peer}, device_id_type=MESH).start())

    def send_last():
        c = n - 1

        @pl.loop(0, subsets)
        def _(r):
            spread(lambda peer: pltpu.make_async_remote_copy(
                src_ref=stage[c].at[pl.ds(peer * piece + r * step, step)],
                dst_ref=recv[c].at[q, pl.ds(r * step, step)],
                send_sem=part_send.at[c], recv_sem=last_recv.at[r],
                device_id={"az": peer}, device_id_type=MESH).start())

    def first_stage(c, r):
        sub = 2 * chunks[c][1]
        flat = recv[c].reshape(az_count * piece * sub, GW)
        x = jnp.concatenate([
            jnp.concatenate(
                [flat[pl.ds((r + k) * sub + s, az_count, stride=piece * sub), :] for s in range(sub)], axis=0)
            for k in range(2)], axis=1)
        x_hi, x_lo = split(x)
        return jnp.dot(
            a_refs[c][...], jnp.concatenate([x_hi, x_lo, x_hi], axis=0), preferred_element_type=jnp.float32)

    def gather_chunk(c):
        table(c).wait()
        others = recv[c].at[pl.ds(0, az_count - 1)]
        pltpu.make_async_copy(others, others, part_recv.at[c]).wait()

        @pl.loop(0, piece // 2)
        def _(i):
            y = first_stage(c, 2 * i)
            y_acc[i] = y if c == 0 else y_acc[i] + y

    def share(src, dst, slot, axis, peer, at):
        return pltpu.make_async_remote_copy(
            src_ref=src, dst_ref=dst.at[slot], send_sem=e_send.at[at],
            recv_sem=e_recv.at[at], device_id={axis: peer}, device_id_type=MESH)

    def share_all(src, dst, slot, axis, count, at):
        dst[slot] = src[...]

        @pl.loop(1, count)
        def _(j):
            share(src, dst, slot, axis, (slot + j) % count, at).start()

    def share_wait(dst, count, at):
        others = dst.at[pl.ds(0, count - 1)]
        pltpu.make_async_copy(others, others, e_send.at[at]).wait()
        pltpu.make_async_copy(others, others, e_recv.at[at]).wait()

    energy = jnp.zeros((8, GW), jnp.float32)
    for c in range(n - 1):
        energy = energy + remap(c)
        send_chunk(c)
        if c >= LAG:
            gather_chunk(c - LAG)
    energy = energy + remap(n - 1)
    e_own[...] = energy
    share_all(e_own, e_az, q, "az", az_count, 0)
    send_last()
    for c in range(max(n - 1 - LAG, 0), n - 1):
        gather_chunk(c)
    share_wait(e_az, az_count, 0)
    e_sum[...] = jnp.sum(e_az[...], axis=0)
    share_all(e_sum, e_rng, p, "rng", rng_count, 1)
    for i in range(n - 1, n + 3):
        table(i).wait()
    share_wait(e_rng, rng_count, 1)
    mean = jnp.sum(jnp.sum(e_rng[...], axis=0), axis=(0, 1), keepdims=True) / cells
    scale = lax.rsqrt(mean + 1e-06)

    halves = total_groups // GW
    nt = (((1,), (1,)), ((), ()))

    @pl.loop(0, subsets)
    def _(s):
        others = recv[n - 1].at[pl.ds(0, az_count - 1), pl.ds(s * step, step)]
        pltpu.make_async_copy(others, others, last_recv.at[s]).wait()
        for k in range(step // 2):
            first = s * step + 2 * k
            y = y_acc[s * (step // 2) + k] + first_stage(n - 1, first)
            t_re, t_im = twist_ref[0], twist_ref[1]
            turned = []
            for i in range(2):
                y_re = y[:total_groups, i * GW:(i + 1) * GW]
                y_im = y[total_groups:, i * GW:(i + 1) * GW]
                turned.append(jnp.concatenate([y_re * t_re - y_im * t_im, y_re * t_im + y_im * t_re], axis=1))
            z_hi, z_lo = split(jnp.concatenate(turned, axis=0) * scale)
            v = (
                lax.dot_general(b_hi_ref[...], z_hi, nt, preferred_element_type=jnp.float32)
                + lax.dot_general(b_hi_ref[...], z_lo, nt, preferred_element_type=jnp.float32)
                + lax.dot_general(b_lo_ref[...], z_hi, nt, preferred_element_type=jnp.float32)
            )
            for i in range(2):
                for c in range(2):
                    for h in range(halves):
                        image_ref[first + i, pl.ds(2 * h + c, GW, stride=2 * halves), :] = (
                            v[c * GW:(c + 1) * GW, i * total_groups + h * GW:i * total_groups + (h + 1) * GW])

    for c in range(n):
        sent = stage[c].at[pl.ds(0, rows - piece)]
        pltpu.make_async_copy(sent, sent, part_send.at[c]).wait()
    for g in range(groups):
        for i in reach:
            pl.when(p >= i + 1)(lambda g=g, i=i: halo(g, i).wait_send())


def fused(spec, src, offsets, weights, tables, chunks, counts, rng_count, az_count):
    rows, groups = spec.shape[:2]
    blocks = rows // BLOCK
    piece = rows // az_count
    step = min(STEP, piece)
    n = len(chunks)
    total_groups = groups * az_count
    cells = float(rows * rng_count * total_groups * GW) * float(total_groups * GW)
    hbm = pl.BlockSpec(memory_space=pl.ANY)
    tile = (8, GW)
    dma = pltpu.SemaphoreType.DMA
    vmem = pltpu.VMEM
    f32 = jnp.float32
    return pl.pallas_call(
        functools.partial(fused_kernel, rows, blocks, groups, chunks, counts, step, cells),
        out_shape=vmem((piece, 2 * total_groups, GW), f32),
        in_specs=[pl.BlockSpec(memory_space=pltpu.SMEM)] + [hbm] * (3 + len(tables)),
        out_specs=pl.BlockSpec(memory_space=vmem),
        scratch_shapes=[vmem((rows + sum(counts), 2, GW), f32)] * groups
        + [vmem((rows, per, 2, GW), f32) for _, per in chunks]
        + [vmem((az_count, piece, per, 2, GW), f32) for _, per in chunks]
        + [vmem(t.shape, t.dtype) for t in tables]
        + [
            vmem((piece // 2, 2 * total_groups, 2 * GW), f32),
            vmem(offsets.shape, offsets.dtype),
            vmem(weights.shape, weights.dtype),
            vmem(tile, f32),
            vmem((az_count,) + tile, f32),
            vmem(tile, f32),
            vmem((rng_count,) + tile, f32),
            dma((2,)),
            dma((len(tables),)),
            dma((groups,)),
            dma((groups, len(counts))),
            dma((groups, len(counts))),
            dma((n,)),
            dma((n,)),
            dma((piece // step,)),
            dma((2,)),
            dma((2,)),
        ],
        compiler_params=pltpu.CompilerParams(
            has_side_effects=True, collective_id=0, vmem_limit_bytes=52 * 1024 * 1024),
    )(src, offsets, weights, spec, *tables)


def store_kernel(parts, band_ref, out_ref, sem):
    size = band_ref.shape[0] // parts
    copies = [
        pltpu.make_async_copy(band_ref.at[pl.ds(i * size, size)], out_ref.at[pl.ds(i * size, size)], sem.at[i])
        for i in range(parts)]
    for copy in copies:
        copy.start()
    for copy in copies:
        copy.wait()


def store(band):
    parts = min(8, band.shape[0])
    return pl.pallas_call(
        functools.partial(store_kernel, parts),
        out_shape=jax.ShapeDtypeStruct(band.shape, band.dtype),
        in_specs=[pl.BlockSpec(memory_space=pltpu.VMEM)],
        out_specs=pl.BlockSpec(memory_space=pl.ANY),
        scratch_shapes=[pltpu.SemaphoreType.DMA((parts,))],
        compiler_params=pltpu.CompilerParams(vmem_limit_bytes=1024 * 1024),
    )(band)


def halo_counts(rows_dev, rng_count):
    total = rows_dev * rng_count
    halo = min(rows_dev - BLOCK + SHIFT_B * BLOCK, total - 2 * BLOCK) + WINDOW - rows_dev
    counts = []
    while halo > 0:
        counts.append(min(halo, rows_dev))
        halo -= rows_dev
    return counts


def body(spectrum, src_block, offsets, tap_weights):
    rows_dev = spectrum.shape[0]
    columns = spectrum.shape[2]
    groups = columns // GW
    rng_count = lax.axis_size("rng")
    az_count = lax.axis_size("az")
    rows_after = rows_dev // az_count
    total_len = columns * az_count
    chunks = plan(groups)
    tables = [jnp.asarray(t) for t in dft_tables(az_count, groups, chunks)]
    spec = spectrum.reshape(rows_dev, 2, groups, GW).transpose(0, 2, 1, 3)
    counts = halo_counts(rows_dev, rng_count)
    band = fused(spec, src_block.T, offsets, tap_weights, tables, chunks, counts, rng_count, az_count)
    image = store(band)
    return (
        image.reshape(rows_after, total_len // GW, 2, GW)
        .transpose(0, 2, 1, 3)
        .reshape(rows_after, 2, total_len)
    )


def solution(mesh):
    placed = (P("rng", None, "az"), P("az", "rng"), P("az", "rng"), P(None, "az", "rng"))
    return jax.shard_map(
        body, mesh=mesh, in_specs=placed, out_specs=P(("rng", "az"), None, None), check_vma=False
    )
```

time: 245 us -> 207 us (0.84)
  Pallas kernels: 241 us -> 207 us
    pallas_call x2, Pallas kernels: 241 us -> 207 us  [the longest x1 204 us: fused(): pl.pallas_call(functools.partial(fused_kernel, rows, blocks, groups, chun...]
where the time goes in v1:
time: 207 us
  Pallas kernels  207 us (100%)
    pallas_call x1, Pallas kernels, fused(): pl.pallas_call(functools.partial(fused_kernel, rows, blocks, groups, chun...  204 us

profile of v1, /device:TPU:0, one launch (start us, length us, event | category | flops | bytes accessed | tf_op | source)
XLA Modules:
  0.0 207.3 jit_solution(8494446525599338952)
XLA Ops:
  0.0 203.9 %shard_map.163.band_ref = f32[32,512,128]{2,1,0:T(8,128)S(1)} custom-call(s32[4,16]{1,0:T(4,128)} %bitcast.10, s32[16,512]{1,0:T(8,128)} %off_hbm.1, f32[8,16,512]{2,1,0:T(8,128)} %w_hbm.1, f32[512,16,2,128]{3,2,1,0:T(2,128)} %bitcast.9, bf16[512,96]{1,0:T(8,128)(2,1)} %constant.26.clone.rest_0_, bf16[512,96]{1,0:T(8,128)(2,1)} %constant.27.clone.rest_1_, ...), custom_call_target="tpu_custom_call" | custom-call | tf_op jit(solution)/shard_map/pallas_call | solution.py:314
  203.9 3.4 %shard_map.164 = f32[32,512,128]{2,1,0:T(8,128)} custom-call(f32[32,512,128]{2,1,0:T(8,128)S(1)} %shard_map.163.band_ref), custom_call_target="tpu_custom_call" | custom-call | tf_op jit(solution)/shard_map/pallas_call | solution.py:360

commit v2 on v1

v2 whole, which is shorter than its diff:
```python
import functools

import jax
import jax.numpy as jnp
import numpy as np
from jax import lax
from jax.experimental import pallas as pl
from jax.experimental.pallas import tpu as pltpu
from jax.sharding import PartitionSpec as P

BLOCK = 128
GW = 128
TAPS = 8
SHIFT_B = 5
WINDOW = 144
LAG = 2
STEP = 4

MESH = pl.DeviceIdType.MESH


def split_np(x):
    hi = x.astype(jnp.bfloat16)
    lo = (x - hi.astype(np.float64)).astype(jnp.bfloat16)
    return hi, lo


def split(x):
    hi = x.astype(jnp.bfloat16)
    lo = (x - hi.astype(jnp.float32)).astype(jnp.bfloat16)
    return hi, lo


def plan(groups):
    last = max(1, groups // 4)
    single = min(groups - last, (3 * groups) // 8)
    sizes = ([1, 1] if single else []) + [2] * (single - 1)
    left = groups - last - single
    sizes += [4] * (left // 2) + [2] * (left % 2) + [2 * last]
    starts = [sum(sizes[:i]) for i in range(len(sizes))]
    return tuple(zip(starts, sizes))


def units_of(chunks):
    units = []
    for c, (start, size) in enumerate(chunks):
        width = min(size, 2)
        units += [(c, at, width) for at in range(0, size, width)]
    return tuple(units)


def dft_tables(az_count, groups, chunks):
    total_groups = az_count * groups
    total_len = total_groups * GW
    k1 = np.arange(total_groups)
    gl, az = np.meshgrid(np.arange(groups), np.arange(az_count), indexing="ij")
    angle = 2.0 * np.pi * ((k1[:, None, None] * (az * groups + gl)[None]) % total_groups) / total_groups
    first = np.empty((2, total_groups, groups, 2, az_count))
    first[0, :, :, 0] = np.cos(angle)
    first[0, :, :, 1] = -np.sin(angle)
    first[1, :, :, 0] = np.sin(angle)
    first[1, :, :, 1] = np.cos(angle)
    first = first.reshape(2 * total_groups, 2 * groups, az_count)
    stage_one = []
    for start, size in chunks:
        hi, lo = split_np(first[:, start:start + size].reshape(2 * total_groups, size * az_count))
        stage_one.append(np.concatenate([hi, hi, lo], axis=1))
    l = np.arange(GW)
    turn = 2.0 * np.pi * (k1[:, None] * l[None, :]) / total_len
    twist = np.stack([np.cos(turn), np.sin(turn)]).astype(np.float32) / np.float32(total_len)
    inner = 2.0 * np.pi * ((l[:, None] * l[None, :]) % GW) / GW
    second = np.empty((2, GW, 2, GW))
    second[0, :, 0] = np.cos(inner)
    second[0, :, 1] = -np.sin(inner)
    second[1, :, 0] = np.sin(inner)
    second[1, :, 1] = np.cos(inner)
    b_hi, b_lo = split_np(second.reshape(2 * GW, 2 * GW))
    return stage_one + [twist, b_hi, b_lo]


def remap_block(ext, width, out, sub, at, b, src, off, weight_row):
    source = [ext[pl.ds(src * (BLOCK * width) + c, WINDOW, stride=width), :] for c in range(width)]
    source = jnp.concatenate(source, axis=1) if width > 1 else source[0]
    where = lax.broadcasted_iota(jnp.int32, (WINDOW, BLOCK), 0) - off
    taps = jnp.zeros((WINDOW, BLOCK), jnp.float32)
    for t in range(TAPS):
        taps = jnp.where(where == t, weight_row(t), taps)
    t_hi, t_lo = split(taps)
    s_hi, s_lo = split(source)
    left = jnp.concatenate([t_hi, t_lo, t_hi], axis=0)
    right = jnp.concatenate([s_hi, s_hi, s_lo], axis=0)
    value = lax.dot_general(
        left, right, (((0,), (0,)), ((), ())), preferred_element_type=jnp.float32
    )
    energy = jnp.zeros((8, GW), jnp.float32)
    for c in range(width):
        half = value[:, c * GW:(c + 1) * GW]
        out[pl.ds(b * BLOCK * sub + at + c, BLOCK, stride=sub), :] = half
        energy = energy + jnp.sum((half * half).reshape(BLOCK // 8, 8, GW), axis=0)
    return energy


def first_stage(recv, a_ref, sub, piece, az_count, row, stored_rows):
    flat = recv.reshape(az_count * stored_rows * sub, GW)
    x = jnp.concatenate([
        jnp.concatenate(
            [flat[pl.ds((row + k) * sub + s, az_count, stride=stored_rows * sub), :] for s in range(sub)], axis=0)
        for k in range(2)], axis=1)
    x_hi, x_lo = split(x)
    return jnp.dot(
        a_ref[...], jnp.concatenate([x_hi, x_lo, x_hi], axis=0), preferred_element_type=jnp.float32)


def second_stage(y, scale, twist_ref, b_hi_ref, b_lo_ref, store):
    total_groups = y.shape[0] // 2
    halves = total_groups // GW
    nt = (((1,), (1,)), ((), ()))
    t_re, t_im = twist_ref[0], twist_ref[1]
    turned = []
    for i in range(2):
        y_re = y[:total_groups, i * GW:(i + 1) * GW]
        y_im = y[total_groups:, i * GW:(i + 1) * GW]
        turned.append(jnp.concatenate([y_re * t_re - y_im * t_im, y_re * t_im + y_im * t_re], axis=1))
    z_hi, z_lo = split(jnp.concatenate(turned, axis=0) * scale)
    v = (
        lax.dot_general(b_hi_ref[...], z_hi, nt, preferred_element_type=jnp.float32)
        + lax.dot_general(b_hi_ref[...], z_lo, nt, preferred_element_type=jnp.float32)
        + lax.dot_general(b_lo_ref[...], z_hi, nt, preferred_element_type=jnp.float32)
    )
    for i in range(2):
        for c in range(2):
            for h in range(halves):
                store(i, pl.ds(2 * h + c, GW, stride=2 * halves),
                      v[c * GW:(c + 1) * GW, i * total_groups + h * GW:i * total_groups + (h + 1) * GW])


def fused_kernel(rows, blocks, chunks, units, counts, step, cells, src_hbm, off_hbm, w_hbm, spec_ref, *rest):
    n = len(chunks)
    tables_hbm, rest = rest[:n + 3], rest[n + 3:]
    image_ref, y_acc, last_recv_ref, scale_ref, a_last, twist_ref, b_hi_ref, b_lo_ref = rest[:8]
    scratch = rest[8:]
    ext, scratch = scratch[:len(units)], scratch[len(units):]
    stage, scratch = scratch[:n], scratch[n:]
    recv, scratch = scratch[:n - 1] + (last_recv_ref,), scratch[n - 1:]
    a_refs, scratch = scratch[:n - 1] + (a_last,), scratch[n - 1:]
    tables = a_refs + (twist_ref, b_hi_ref, b_lo_ref)
    (src_ref, off_ref, w_ref, e_own, e_az, e_sum, e_rng, small_sem, table_sem, local_sem, halo_send, halo_recv,
     part_send, part_recv, last_recv, e_send, e_recv) = scratch
    rng_count, az_count = lax.axis_size("rng"), lax.axis_size("az")
    p, q = lax.axis_index("rng"), lax.axis_index("az")
    piece = rows // az_count
    half = max(az_count // 2, 1)
    side, place = q // half, q % half
    subsets = piece // step
    reach = [i for i in range(len(counts)) if i + 1 < rng_count]

    barrier = pltpu.get_barrier_semaphore()

    @pl.loop(1, rng_count)
    def _(j):
        pl.semaphore_signal(barrier, inc=1, device_id={"rng": (p + j) % rng_count}, device_id_type=MESH)

    @pl.loop(1, az_count)
    def _(j):
        pl.semaphore_signal(barrier, inc=1, device_id={"az": (q + j) % az_count}, device_id_type=MESH)

    def column(u):
        c, at, width = units[u]
        return pl.ds(chunks[c][0] + at, width)

    def local(u):
        return pltpu.make_async_copy(
            spec_ref.at[:, column(u)], ext[u].at[pl.ds(0, rows)], local_sem.at[u])

    def halo(u, i):
        source = ext[u].at[pl.ds(0, counts[i])] if u == 0 else spec_ref.at[pl.ds(0, counts[i]), column(u)]
        return pltpu.make_async_remote_copy(
            src_ref=source,
            dst_ref=ext[u].at[pl.ds(rows + sum(counts[:i]), counts[i])],
            send_sem=halo_send.at[u, i], recv_sem=halo_recv.at[u, i],
            device_id={"rng": (p + rng_count - i - 1) % rng_count}, device_id_type=MESH)

    def table(i):
        return pltpu.make_async_copy(tables_hbm[i], tables[i], table_sem.at[i])

    local(0).start()
    small = [pltpu.make_async_copy(hbm, ref, small_sem.at[i])
             for i, (hbm, ref) in enumerate(((src_hbm, src_ref), (off_hbm, off_ref), (w_hbm, w_ref)))]
    for copy in small:
        copy.start()
    for u in range(1, len(units)):
        local(u).start()
    for i in range(n + 3):
        table(i).start()
    local(0).wait()
    pl.semaphore_wait(barrier, rng_count + az_count - 2)

    for u in range(len(units)):
        for i in reach:
            pl.when(p >= i + 1)(lambda u=u, i=i: halo(u, i).start())
    for copy in small:
        copy.wait()

    def arrive(u):
        if u:
            local(u).wait()
        for i in reach:
            pl.when(p + i + 1 < rng_count)(lambda: halo(u, i).wait_recv())

    def remap(u, b):
        c, at, width = units[u]
        g, sub = (chunks[c][0] + at) // 2, chunks[c][1]
        lanes = pl.ds(b * BLOCK if isinstance(b, int) else pl.multiple_of(b * BLOCK, BLOCK), BLOCK)
        return remap_block(
            ext[u].reshape(ext[u].shape[0] * width, GW), width, stage[c].reshape(rows * sub, GW), sub, at, b,
            jnp.maximum(src_ref[b, g] - p * blocks, 0), off_ref[pl.ds(g, 1), lanes],
            lambda t: w_ref[t, pl.ds(g, 1), lanes])

    def keep(c):
        recv[c][q] = stage[c][pl.ds(q * piece, piece)]

    def remap_chunk(c):
        energy = jnp.zeros((8, GW), jnp.float32)
        for u in range(len(units)):
            if units[u][0] == c:
                arrive(u)
                for b in range(blocks):
                    energy = energy + remap(u, b)
        keep(c)
        return energy

    def spread(send):
        @pl.loop(0, half)
        def _(j):
            send((1 - side) * half + (place + j) % half)

        @pl.loop(1, half)
        def _(j):
            send(side * half + (place + j) % half)

    def send_piece(c, peer):
        pltpu.make_async_remote_copy(
            src_ref=stage[c].at[pl.ds(peer * piece, piece)],
            dst_ref=recv[c].at[q],
            send_sem=part_send.at[c], recv_sem=part_recv.at[c],
            device_id={"az": peer}, device_id_type=MESH).start()

    def first_chunk():
        peers = BLOCK // piece
        energy = jnp.zeros((8, GW), jnp.float32)
        arrive(0)
        for k in range(blocks):
            b = (k + (1 - side) * (blocks // 2)) % blocks
            energy = energy + remap(0, b)

            @pl.loop(0, peers)
            def _(j):
                peer = b * peers + (place + j) % peers
                pl.when(peer != q)(lambda: send_piece(0, peer))

        keep(0)
        return energy

    def send_last():
        c = n - 1

        @pl.loop(0, subsets)
        def _(r):
            spread(lambda peer: pltpu.make_async_remote_copy(
                src_ref=stage[c].at[pl.ds(peer * piece + r * step, step)],
                dst_ref=recv[c].at[q, pl.ds(r * step, step)],
                send_sem=part_send.at[c], recv_sem=last_recv.at[r],
                device_id={"az": peer}, device_id_type=MESH).start())

    def rows_of(c, row):
        return first_stage(recv[c], a_refs[c], chunks[c][1], piece, az_count, row, piece)

    def gather_chunk(c):
        table(c).wait()
        others = recv[c].at[pl.ds(0, az_count - 1)]
        pltpu.make_async_copy(others, others, part_recv.at[c]).wait()

        @pl.loop(0, piece // 2)
        def _(i):
            y = rows_of(c, 2 * i)
            y_acc[i] = y if c == 0 else y_acc[i] + y

    def share(src, dst, slot, axis, peer, at):
        return pltpu.make_async_remote_copy(
            src_ref=src, dst_ref=dst.at[slot], send_sem=e_send.at[at],
            recv_sem=e_recv.at[at], device_id={axis: peer}, device_id_type=MESH)

    def share_all(src, dst, slot, axis, count, at):
        dst[slot] = src[...]

        @pl.loop(1, count)
        def _(j):
            share(src, dst, slot, axis, (slot + j) % count, at).start()

    def share_wait(dst, count, at):
        others = dst.at[pl.ds(0, count - 1)]
        pltpu.make_async_copy(others, others, e_send.at[at]).wait()
        pltpu.make_async_copy(others, others, e_recv.at[at]).wait()

    energy = first_chunk()
    for c in range(1, n - 1):
        energy = energy + remap_chunk(c)
        spread(functools.partial(send_piece, c))
        if c >= LAG:
            gather_chunk(c - LAG)
    energy = energy + remap_chunk(n - 1)
    e_own[...] = energy
    share_all(e_own, e_az, q, "az", az_count, 0)
    send_last()
    for c in range(max(n - 1 - LAG, 0), n - 1):
        gather_chunk(c)
    share_wait(e_az, az_count, 0)
    e_sum[...] = jnp.sum(e_az[...], axis=0)
    share_all(e_sum, e_rng, p, "rng", rng_count, 1)
    for i in range(n - 1, n + 3):
        table(i).wait()
    share_wait(e_rng, rng_count, 1)
    mean = jnp.sum(jnp.sum(e_rng[...], axis=0), axis=(0, 1), keepdims=True) / cells
    scale = lax.rsqrt(mean + 1e-06)
    scale_ref[...] = jnp.broadcast_to(scale, scale_ref.shape)

    def arrived(s):
        others = recv[n - 1].at[pl.ds(0, az_count - 1), pl.ds(s * step, step)]
        pltpu.make_async_copy(others, others, last_recv.at[s]).wait()

    @pl.loop(0, subsets - 1)
    def _(s):
        arrived(s)
        for k in range(step // 2):
            first = s * step + 2 * k
            y = y_acc[s * (step // 2) + k] + rows_of(n - 1, first)

            def store(i, lines, value):
                image_ref[first + i, lines, :] = value

            second_stage(y, scale, twist_ref, b_hi_ref, b_lo_ref, store)

    for c in range(n):
        sent = stage[c].at[pl.ds(0, rows - piece)]
        pltpu.make_async_copy(sent, sent, part_send.at[c]).wait()
    for u in range(len(units)):
        for i in reach:
            pl.when(p >= i + 1)(lambda u=u, i=i: halo(u, i).wait_send())
    arrived(subsets - 1)


def fused(spec, src, offsets, weights, tables, chunks, counts, step, rng_count, az_count):
    rows, columns = spec.shape[:2]
    blocks = rows // BLOCK
    piece = rows // az_count
    n = len(chunks)
    units = units_of(chunks)
    total_groups = columns // 2 * az_count
    cells = float(rows * rng_count * total_groups * GW) * float(total_groups * GW)
    hbm = pl.BlockSpec(memory_space=pl.ANY)
    tile = (8, GW)
    dma = pltpu.SemaphoreType.DMA
    vmem = pltpu.VMEM
    f32 = jnp.float32
    sizes = [size for _, size in chunks]
    outs = [
        vmem(((piece - step), 2 * total_groups, GW), f32),
        vmem((piece // 2, 2 * total_groups, 2 * GW), f32),
        vmem((az_count, piece, sizes[-1], 1, GW), f32),
        vmem(tile, f32),
    ] + [vmem(t.shape, t.dtype) for t in tables[n - 1:]]
    return pl.pallas_call(
        functools.partial(fused_kernel, rows, blocks, chunks, units, counts, step, cells),
        out_shape=outs,
        in_specs=[hbm] * (4 + len(tables)),
        out_specs=[pl.BlockSpec(memory_space=vmem)] * len(outs),
        scratch_shapes=[vmem((rows + sum(counts), width, 1, GW), f32) for _, _, width in units]
        + [vmem((rows, size, 1, GW), f32) for size in sizes]
        + [vmem((az_count, piece, size, 1, GW), f32) for size in sizes[:-1]]
        + [vmem(t.shape, t.dtype) for t in tables[:n - 1]]
        + [
            pltpu.SMEM(src.shape, src.dtype),
            vmem(offsets.shape, offsets.dtype),
            vmem(weights.shape, weights.dtype),
            vmem(tile, f32),
            vmem((az_count,) + tile, f32),
            vmem(tile, f32),
            vmem((rng_count,) + tile, f32),
            dma((3,)),
            dma((len(tables),)),
            dma((len(units),)),
            dma((len(units), len(counts))),
            dma((len(units), len(counts))),
            dma((n,)),
            dma((n,)),
            dma((piece // step,)),
            dma((2,)),
            dma((2,)),
        ],
        compiler_params=pltpu.CompilerParams(
            has_side_effects=True, collective_id=0, vmem_limit_bytes=40 * 1024 * 1024),
    )(src, offsets, weights, spec, *tables)


def store_kernel(step, band_ref, y_acc, recv, scale_ref, a_ref, twist_ref, b_hi_ref, b_lo_ref, out_ref, end, sem):
    done = band_ref.shape[0]
    parts = done // step
    az_count, piece, sub = recv.shape[:3]

    def copy(i):
        source = band_ref.at[pl.ds(i * step, step)] if i < parts else end
        return pltpu.make_async_copy(source, out_ref.at[pl.ds(i * step, step)], sem.at[i])

    for i in range(parts):
        copy(i).start()
    for k in range(step // 2):
        first = done + 2 * k
        y = y_acc[first // 2] + first_stage(recv, a_ref, sub, piece, az_count, first, piece)

        def store(i, lines, value, k=k):
            end[2 * k + i, lines, :] = value

        second_stage(y, scale_ref[:1, :1], twist_ref, b_hi_ref, b_lo_ref, store)
    copy(parts).start()
    for i in range(parts + 1):
        copy(i).wait()


def store(step, rows, band, *rest):
    parts = rows // step
    vmem = pltpu.VMEM
    return pl.pallas_call(
        functools.partial(store_kernel, step),
        out_shape=jax.ShapeDtypeStruct((rows,) + band.shape[1:], band.dtype),
        in_specs=[pl.BlockSpec(memory_space=vmem)] * (1 + len(rest)),
        out_specs=pl.BlockSpec(memory_space=pl.ANY),
        scratch_shapes=[vmem((step,) + band.shape[1:], band.dtype), pltpu.SemaphoreType.DMA((parts,))],
        compiler_params=pltpu.CompilerParams(vmem_limit_bytes=12 * 1024 * 1024),
    )(band, *rest)


def halo_counts(rows_dev, rng_count):
    total = rows_dev * rng_count
    halo = min(rows_dev - BLOCK + SHIFT_B * BLOCK, total - 2 * BLOCK) + WINDOW - rows_dev
    counts = []
    while halo > 0:
        counts.append(min(halo, rows_dev))
        halo -= rows_dev
    return counts


def body(spectrum, src_block, offsets, tap_weights):
    rows_dev = spectrum.shape[0]
    columns = spectrum.shape[2]
    groups = columns // GW
    rng_count = lax.axis_size("rng")
    az_count = lax.axis_size("az")
    rows_after = rows_dev // az_count
    total_len = columns * az_count
    chunks = plan(groups)
    tables = [jnp.asarray(t) for t in dft_tables(az_count, groups, chunks)]
    spec = spectrum.reshape(rows_dev, 2, groups, GW).transpose(0, 2, 1, 3).reshape(rows_dev, 2 * groups, 1, GW)
    counts = halo_counts(rows_dev, rng_count)
    step = min(STEP, rows_after // 2)
    held = fused(spec, src_block.T, offsets, tap_weights, tables, chunks, counts, step, rng_count, az_count)
    image = store(step, rows_after, *held)
    return (
        image.reshape(rows_after, total_len // GW, 2, GW)
        .transpose(0, 2, 1, 3)
        .reshape(rows_after, 2, total_len)
    )


def solution(mesh):
    placed = (P("rng", None, "az"), P("az", "rng"), P("az", "rng"), P(None, "az", "rng"))
    return jax.shard_map(
        body, mesh=mesh, in_specs=placed, out_specs=P(("rng", "az"), None, None), check_vma=False
    )
```

time: 207 us -> 203 us (0.981)
  Pallas kernels: 207 us -> 202 us
    pallas_call x2, Pallas kernels: 207 us -> 202 us  [the longest x1 199 us: fused(): pl.pallas_call(functools.partial(fused_kernel, rows, blocks, chunks, unit...]
where the time goes in v2:
time: 203 us; the launch traced here: 202 us
  Pallas kernels  202 us (100%)
    pallas_call x1, Pallas kernels, fused(): pl.pallas_call(functools.partial(fused_kernel, rows, blocks, chunks, unit...  199 us

profile of v2, /device:TPU:0, one launch (start us, length us, event | category | flops | bytes accessed | tf_op | source)
XLA Modules:
  0.0 202.5 jit_solution(16409299474293011117)
XLA Ops:
  0.0 198.8 %shard_map.172 = (f32[28,512,128]{2,1,0:T(8,128)S(1)}, f32[16,512,256]{2,1,0:T(8,128)S(1)}, f32[16,32,8,1,128]{4,3,2,1,0:T(1,128)S(1)}, f32[8,128]{1,0:T(8,128)S...) custom-call(s32[4,16]{1,0:T(4,128)} %bitcast.12, ...), custom_call_target="tpu_custom_call" | custom-call | tf_op jit(solution)/shard_map/pallas_call | solution.py:372
  198.8 3.7 %shard_map.173 = f32[32,512,128]{2,1,0:T(8,128)} custom-call(f32[28,512,128]{2,1,0:T(8,128)S(1)} %get-tuple-element.13.band_ref, f32[16,512,256]{2,1,0:T(8,128)S(1)} %get-tuple-element.14.y_acc, f32[16,32,8,1,128]{4,3,2,1,0:T(1,128)S(1)} %get-tuple-element.15.recv, f32[8,128]{1,0:T(8,128)S(1)} %get-tuple-element.16.scale_ref, ...), custom_call_target="tpu_custom_call" | custom-call | tf_op jit(solution)/shard_map/pallas_call | solution.py:432

commit v3 on v2

--- a/solution.py
+++ b/solution.py
@@ -14,6 +14,8 @@
 SHIFT_B = 5
 WINDOW = 144
 LAG = 2
+RELAY = 1
+RELAY_AT = 4
 STEP = 4
 
 MESH = pl.DeviceIdType.MESH
@@ -145,7 +147,7 @@
     a_refs, scratch = scratch[:n - 1] + (a_last,), scratch[n - 1:]
     tables = a_refs + (twist_ref, b_hi_ref, b_lo_ref)
     (src_ref, off_ref, w_ref, e_own, e_az, e_sum, e_rng, small_sem, table_sem, local_sem, halo_send, halo_recv,
-     part_send, part_recv, last_recv, e_send, e_recv) = scratch
+     part_send, part_recv, last_recv, e_send, e_recv, relay_sem, *relay) = scratch
     rng_count, az_count = lax.axis_size("rng"), lax.axis_size("az")
     p, q = lax.axis_index("rng"), lax.axis_index("az")
     piece = rows // az_count
@@ -188,16 +190,16 @@
              for i, (hbm, ref) in enumerate(((src_hbm, src_ref), (off_hbm, off_ref), (w_hbm, w_ref)))]
     for copy in small:
         copy.start()
+    local(0).wait()
+    pl.semaphore_wait(barrier, rng_count + az_count - 2)
+
+    for u in range(len(units)):
+        for i in reach:
+            pl.when(p >= i + 1)(lambda u=u, i=i: halo(u, i).start())
     for u in range(1, len(units)):
         local(u).start()
     for i in range(n + 3):
         table(i).start()
-    local(0).wait()
-    pl.semaphore_wait(barrier, rng_count + az_count - 2)
-
-    for u in range(len(units)):
-        for i in reach:
-            pl.when(p >= i + 1)(lambda u=u, i=i: halo(u, i).start())
     for copy in small:
         copy.wait()
 
@@ -245,6 +247,50 @@
             send_sem=part_send.at[c], recv_sem=part_recv.at[c],
             device_id={"az": peer}, device_id_type=MESH).start()
 
+    def hand_over(peer):
+        pltpu.make_async_remote_copy(
+            src_ref=stage[RELAY].at[pl.ds(peer * piece, piece)],
+            dst_ref=relay[0].at[peer % half // 2],
+            send_sem=relay_sem.at[0], recv_sem=relay_sem.at[1],
+            device_id={"rng": 1 - p}, device_id_type=MESH).start()
+
+    def send_relayed():
+        @pl.loop(0, half)
+        def _(j):
+            peer = (1 - side) * half + (place + j) % half
+            via = (p == 0) & (peer % 2 == 0)
+            pl.when(via)(lambda: hand_over(peer))
+            pl.when(jnp.logical_not(via))(lambda: send_piece(RELAY, peer))
+
+        @pl.loop(1, half)
+        def _(j):
+            send_piece(RELAY, side * half + (place + j) % half)
+
+    def forward():
+        pltpu.make_async_copy(relay[0], relay[0], relay_sem.at[1]).wait()
+
+        @pl.loop(0, half // 2)
+        def _(i):
+            pltpu.make_async_remote_copy(
+                src_ref=relay[0].at[i],
+                dst_ref=recv[RELAY].at[q],
+                send_sem=relay_sem.at[2], recv_sem=part_recv.at[RELAY],
+                device_id={"rng": 1 - p, "az": (1 - side) * half + 2 * i}, device_id_type=MESH).start()
+
+    def relay_done():
+        def handed():
+            sent = stage[RELAY].at[pl.ds(0, rows - piece - half // 2 * piece)]
+            pltpu.make_async_copy(sent, sent, part_send.at[RELAY]).wait()
+            pltpu.make_async_copy(relay[0], relay[0], relay_sem.at[0]).wait()
+
+        def forwarded():
+            sent = stage[RELAY].at[pl.ds(0, rows - piece)]
+            pltpu.make_async_copy(sent, sent, part_send.at[RELAY]).wait()
+            pltpu.make_async_copy(relay[0], relay[0], relay_sem.at[2]).wait()
+
+        pl.when(p == 0)(handed)
+        pl.when(p != 0)(forwarded)
+
     def first_chunk():
         peers = BLOCK // piece
         energy = jnp.zeros((8, GW), jnp.float32)
@@ -305,15 +351,22 @@
     energy = first_chunk()
     for c in range(1, n - 1):
         energy = energy + remap_chunk(c)
-        spread(functools.partial(send_piece, c))
-        if c >= LAG:
+        if relay and c == RELAY:
+            send_relayed()
+        else:
+            spread(functools.partial(send_piece, c))
+        if c >= LAG and not (relay and c - LAG == RELAY):
             gather_chunk(c - LAG)
+        if relay and c == RELAY_AT:
+            pl.when(p != 0)(forward)
     energy = energy + remap_chunk(n - 1)
     e_own[...] = energy
     share_all(e_own, e_az, q, "az", az_count, 0)
     send_last()
     for c in range(max(n - 1 - LAG, 0), n - 1):
         gather_chunk(c)
+    if relay:
+        gather_chunk(RELAY)
     share_wait(e_az, az_count, 0)
     e_sum[...] = jnp.sum(e_az[...], axis=0)
     share_all(e_sum, e_rng, p, "rng", rng_count, 1)
@@ -341,6 +394,9 @@
             second_stage(y, scale, twist_ref, b_hi_ref, b_lo_ref, store)
 
     for c in range(n):
+        if relay and c == RELAY:
+            relay_done()
+            continue
         sent = stage[c].at[pl.ds(0, rows - piece)]
         pltpu.make_async_copy(sent, sent, part_send.at[c]).wait()
     for u in range(len(units)):
@@ -363,6 +419,9 @@
     vmem = pltpu.VMEM
     f32 = jnp.float32
     sizes = [size for _, size in chunks]
+    relays = []
+    if rng_count == 2 and az_count % 4 == 0 and n - 1 - LAG > RELAY_AT and sizes[RELAY] == 1:
+        relays = [vmem((az_count // 4, piece, 1, 1, GW), f32)]
     outs = [
         vmem(((piece - step), 2 * total_groups, GW), f32),
         vmem((piece // 2, 2 * total_groups, 2 * GW), f32),
@@ -396,34 +455,43 @@
             dma((piece // step,)),
             dma((2,)),
             dma((2,)),
-        ],
+            dma((3,)),
+        ] + relays,
         compiler_params=pltpu.CompilerParams(
             has_side_effects=True, collective_id=0, vmem_limit_bytes=40 * 1024 * 1024),
     )(src, offsets, weights, spec, *tables)
 
 
-def store_kernel(step, band_ref, y_acc, recv, scale_ref, a_ref, twist_ref, b_hi_ref, b_lo_ref, out_ref, end, sem):
+def store_kernel(step, band_ref, y_acc, recv, scale_ref, a_ref, twist_ref, b_hi_ref, b_lo_ref, out_ref, end, sem, end_sem):
     done = band_ref.shape[0]
     parts = done // step
     az_count, piece, sub = recv.shape[:3]
 
     def copy(i):
-        source = band_ref.at[pl.ds(i * step, step)] if i < parts else end
-        return pltpu.make_async_copy(source, out_ref.at[pl.ds(i * step, step)], sem.at[i])
+        rows = pl.ds(i * step, step)
+        return pltpu.make_async_copy(band_ref.at[rows], out_ref.at[rows], sem.at[i])
+
+    def copy_end(k):
+        return pltpu.make_async_copy(end.at[pl.ds(2 * k, 2)], out_ref.at[pl.ds(done + 2 * k, 2)], end_sem.at[k])
 
     for i in range(parts):
         copy(i).start()
-    for k in range(step // 2):
+
+    @pl.loop(0, step // 2)
+    def _(k):
         first = done + 2 * k
         y = y_acc[first // 2] + first_stage(recv, a_ref, sub, piece, az_count, first, piece)
 
-        def store(i, lines, value, k=k):
+        def store(i, lines, value):
             end[2 * k + i, lines, :] = value
 
         second_stage(y, scale_ref[:1, :1], twist_ref, b_hi_ref, b_lo_ref, store)
-    copy(parts).start()
-    for i in range(parts + 1):
+        copy_end(k).start()
+
+    for i in range(parts):
         copy(i).wait()
+    for k in range(step // 2):
+        copy_end(k).wait()
 
 
 def store(step, rows, band, *rest):
@@ -434,7 +502,8 @@
         out_shape=jax.ShapeDtypeStruct((rows,) + band.shape[1:], band.dtype),
         in_specs=[pl.BlockSpec(memory_space=vmem)] * (1 + len(rest)),
         out_specs=pl.BlockSpec(memory_space=pl.ANY),
-        scratch_shapes=[vmem((step,) + band.shape[1:], band.dtype), pltpu.SemaphoreType.DMA((parts,))],
+        scratch_shapes=[vmem((step,) + band.shape[1:], band.dtype), pltpu.SemaphoreType.DMA((parts - 1,)),
+                        pltpu.SemaphoreType.DMA((step // 2,))],
         compiler_params=pltpu.CompilerParams(vmem_limit_bytes=12 * 1024 * 1024),
     )(band, *rest)
 

time: 203 us -> 203 us (level)
  no operation moved by 1% of the time
where the time goes in v3:
time: 203 us; the launch traced here: 202 us
  Pallas kernels  202 us (100%)
    pallas_call x1, Pallas kernels, fused(): pl.pallas_call(functools.partial(fused_kernel, rows, blocks, chunks, unit...  199 us

profile of v3, /device:TPU:0, one launch (start us, length us, event | category | flops | bytes accessed | tf_op | source)
XLA Modules:
  0.0 202.4 jit_solution(6831051369203453792)
XLA Ops:
  0.0 199.0 %shard_map.172 = (f32[28,512,128]{2,1,0:T(8,128)S(1)}, f32[16,512,256]{2,1,0:T(8,128)S(1)}, f32[16,32,8,1,128]{4,3,2,1,0:T(1,128)S(1)}, f32[8,128]{1,0:T(8,128)S...) custom-call(s32[4,16]{1,0:T(4,128)} %bitcast.12, ...), custom_call_target="tpu_custom_call" | custom-call | tf_op jit(solution)/shard_map/pallas_call | solution.py:431
  199.1 3.4 %shard_map.173 = f32[32,512,128]{2,1,0:T(8,128)} custom-call(f32[28,512,128]{2,1,0:T(8,128)S(1)} %get-tuple-element.13.band_ref, f32[16,512,256]{2,1,0:T(8,128)S(1)} %get-tuple-element.14.y_acc, f32[16,32,8,1,128]{4,3,2,1,0:T(1,128)S(1)} %get-tuple-element.15.recv, f32[8,128]{1,0:T(8,128)S(1)} %get-tuple-element.16.scale_ref, ...), custom_call_target="tpu_custom_call" | custom-call | tf_op jit(solution)/shard_map/pallas_call | solution.py:500

commit v4 on v3

--- a/solution.py
+++ b/solution.py
@@ -13,10 +13,13 @@
 TAPS = 8
 SHIFT_B = 5
 WINDOW = 144
+UNUSED = WINDOW - (BLOCK - 1 + TAPS)
 LAG = 2
-RELAY = 1
-RELAY_AT = 4
+RELAY = 7
+RELAY_AT = 10
 STEP = 4
+PAIRS = 4
+PAD = 1
 
 MESH = pl.DeviceIdType.MESH
 
@@ -34,11 +37,11 @@
 
 
 def plan(groups):
-    last = max(1, groups // 4)
-    single = min(groups - last, (3 * groups) // 8)
-    sizes = ([1, 1] if single else []) + [2] * (single - 1)
-    left = groups - last - single
-    sizes += [4] * (left // 2) + [2] * (left % 2) + [2 * last]
+    last = max(1, 3 * groups // 16)
+    halves = groups // 4
+    left = groups - last - halves
+    pairs = 2 * left // 9
+    sizes = [1] * (2 * halves) + [2] * (left - 2 * pairs) + [4] * pairs + [2 * last]
     starts = [sum(sizes[:i]) for i in range(len(sizes))]
     return tuple(zip(starts, sizes))
 
@@ -51,7 +54,26 @@
     return tuple(units)
 
 
-def dft_tables(az_count, groups, chunks):
+def relays(chunks, rng_count, az_count):
+    return rng_count == 2 and az_count % 4 == 0 and len(chunks) - 1 - LAG > RELAY_AT and chunks[RELAY][1] == 1
+
+
+def gather_sets(chunks, relay):
+    sets, held = [[]], 0
+    for c, (_, size) in enumerate(chunks[:-1]):
+        if relay and c == RELAY:
+            continue
+        if held + size > 4 and sets[-1]:
+            sets.append([])
+            held = 0
+        sets[-1].append(c)
+        held += size
+    if relay:
+        sets[-1].append(RELAY)
+    return tuple(tuple(members) for members in sets) + ((len(chunks) - 1,),)
+
+
+def dft_tables(az_count, groups, chunks, sets):
     total_groups = az_count * groups
     total_len = total_groups * GW
     k1 = np.arange(total_groups)
@@ -64,8 +86,9 @@
     first[1, :, :, 1] = np.cos(angle)
     first = first.reshape(2 * total_groups, 2 * groups, az_count)
     stage_one = []
-    for start, size in chunks:
-        hi, lo = split_np(first[:, start:start + size].reshape(2 * total_groups, size * az_count))
+    for members in sets:
+        columns = [h for c in members for h in range(chunks[c][0], sum(chunks[c]))]
+        hi, lo = split_np(first[:, columns].reshape(2 * total_groups, len(columns) * az_count))
         stage_one.append(np.concatenate([hi, hi, lo], axis=1))
     l = np.arange(GW)
     turn = 2.0 * np.pi * (k1[:, None] * l[None, :]) / total_len
@@ -102,18 +125,21 @@
     return energy
 
 
-def first_stage(recv, a_ref, sub, piece, az_count, row, stored_rows):
-    flat = recv.reshape(az_count * stored_rows * sub, GW)
-    x = jnp.concatenate([
-        jnp.concatenate(
-            [flat[pl.ds((row + k) * sub + s, az_count, stride=stored_rows * sub), :] for s in range(sub)], axis=0)
-        for k in range(2)], axis=1)
-    x_hi, x_lo = split(x)
+def first_stage(parts, a_ref, row):
+    columns = []
+    for k in range(2):
+        lines = []
+        for recv in parts:
+            az_count, stored, sub = recv.shape[:3]
+            flat = recv.reshape(az_count * stored * sub, GW)
+            lines += [flat[pl.ds((row + k) * sub + s, az_count, stride=stored * sub), :] for s in range(sub)]
+        columns.append(jnp.concatenate(lines, axis=0))
+    x_hi, x_lo = split(jnp.concatenate(columns, axis=1))
     return jnp.dot(
         a_ref[...], jnp.concatenate([x_hi, x_lo, x_hi], axis=0), preferred_element_type=jnp.float32)
 
 
-def second_stage(y, scale, twist_ref, b_hi_ref, b_lo_ref, store):
+def second_stage(y, twist_ref, b_hi_ref, b_lo_ref, store):
     total_groups = y.shape[0] // 2
     halves = total_groups // GW
     nt = (((1,), (1,)), ((), ()))
@@ -123,7 +149,7 @@
         y_re = y[:total_groups, i * GW:(i + 1) * GW]
         y_im = y[total_groups:, i * GW:(i + 1) * GW]
         turned.append(jnp.concatenate([y_re * t_re - y_im * t_im, y_re * t_im + y_im * t_re], axis=1))
-    z_hi, z_lo = split(jnp.concatenate(turned, axis=0) * scale)
+    z_hi, z_lo = split(jnp.concatenate(turned, axis=0))
     v = (
         lax.dot_general(b_hi_ref[...], z_hi, nt, preferred_element_type=jnp.float32)
         + lax.dot_general(b_hi_ref[...], z_lo, nt, preferred_element_type=jnp.float32)
@@ -136,15 +162,15 @@
                       v[c * GW:(c + 1) * GW, i * total_groups + h * GW:i * total_groups + (h + 1) * GW])
 
 
-def fused_kernel(rows, blocks, chunks, units, counts, step, cells, src_hbm, off_hbm, w_hbm, spec_ref, *rest):
-    n = len(chunks)
-    tables_hbm, rest = rest[:n + 3], rest[n + 3:]
+def fused_kernel(rows, blocks, chunks, sets, units, counts, step, cells, src_hbm, off_hbm, w_hbm, spec_ref, *rest):
+    n, m = len(chunks), len(sets)
+    tables_hbm, rest = rest[:m + 3], rest[m + 3:]
     image_ref, y_acc, last_recv_ref, scale_ref, a_last, twist_ref, b_hi_ref, b_lo_ref = rest[:8]
     scratch = rest[8:]
     ext, scratch = scratch[:len(units)], scratch[len(units):]
     stage, scratch = scratch[:n], scratch[n:]
     recv, scratch = scratch[:n - 1] + (last_recv_ref,), scratch[n - 1:]
-    a_refs, scratch = scratch[:n - 1] + (a_last,), scratch[n - 1:]
+    a_refs, scratch = scratch[:m - 1] + (a_last,), scratch[m - 1:]
     tables = a_refs + (twist_ref, b_hi_ref, b_lo_ref)
     (src_ref, off_ref, w_ref, e_own, e_az, e_sum, e_rng, small_sem, table_sem, local_sem, halo_send, halo_recv,
      part_send, part_recv, last_recv, e_send, e_recv, relay_sem, *relay) = scratch
@@ -198,8 +224,10 @@
             pl.when(p >= i + 1)(lambda u=u, i=i: halo(u, i).start())
     for u in range(1, len(units)):
         local(u).start()
-    for i in range(n + 3):
+    for i in range(m + 3):
         table(i).start()
+    for u, (_, _, width) in enumerate(units):
+        ext[u][pl.ds(rows + sum(counts), UNUSED)] = jnp.zeros((UNUSED, width, 1, GW), jnp.float32)
     for copy in small:
         copy.wait()
 
@@ -219,15 +247,14 @@
             lambda t: w_ref[t, pl.ds(g, 1), lanes])
 
     def keep(c):
-        recv[c][q] = stage[c][pl.ds(q * piece, piece)]
+        recv[c][q, pl.ds(0, piece)] = stage[c][pl.ds(q * piece, piece)]
 
     def remap_chunk(c):
         energy = jnp.zeros((8, GW), jnp.float32)
         for u in range(len(units)):
             if units[u][0] == c:
                 arrive(u)
-                for b in range(blocks):
-                    energy = energy + remap(u, b)
+                energy = lax.fori_loop(0, blocks, lambda b, e, u=u: e + remap(u, b), energy)
         keep(c)
         return energy
 
@@ -243,7 +270,7 @@
     def send_piece(c, peer):
         pltpu.make_async_remote_copy(
             src_ref=stage[c].at[pl.ds(peer * piece, piece)],
-            dst_ref=recv[c].at[q],
+            dst_ref=recv[c].at[q, pl.ds(0, piece)],
             send_sem=part_send.at[c], recv_sem=part_recv.at[c],
             device_id={"az": peer}, device_id_type=MESH).start()
 
@@ -273,7 +300,7 @@
         def _(i):
             pltpu.make_async_remote_copy(
                 src_ref=relay[0].at[i],
-                dst_ref=recv[RELAY].at[q],
+                dst_ref=recv[RELAY].at[q, pl.ds(0, piece)],
                 send_sem=relay_sem.at[2], recv_sem=part_recv.at[RELAY],
                 device_id={"rng": 1 - p, "az": (1 - side) * half + 2 * i}, device_id_type=MESH).start()
 
@@ -318,18 +345,21 @@
                 send_sem=part_send.at[c], recv_sem=last_recv.at[r],
                 device_id={"az": peer}, device_id_type=MESH).start())
 
-    def rows_of(c, row):
-        return first_stage(recv[c], a_refs[c], chunks[c][1], piece, az_count, row, piece)
-
-    def gather_chunk(c):
-        table(c).wait()
-        others = recv[c].at[pl.ds(0, az_count - 1)]
-        pltpu.make_async_copy(others, others, part_recv.at[c]).wait()
-
-        @pl.loop(0, piece // 2)
-        def _(i):
-            y = rows_of(c, 2 * i)
-            y_acc[i] = y if c == 0 else y_acc[i] + y
+    def rows_of(at, row):
+        return first_stage([recv[c] for c in sets[at]], a_refs[at], row)
+
+    def gather(at):
+        table(at).wait()
+        for c in sets[at]:
+            others = recv[c].at[pl.ds(0, az_count - 1), pl.ds(0, piece)]
+            pltpu.make_async_copy(others, others, part_recv.at[c]).wait()
+        pairs = min(PAIRS, piece // 2)
+
+        @pl.loop(0, piece // 2, step=pairs)
+        def _(first):
+            for k in range(pairs):
+                y = rows_of(at, 2 * (first + k))
+                y_acc[first + k] = y if at == 0 else y_acc[first + k] + y
 
     def share(src, dst, slot, axis, peer, at):
         return pltpu.make_async_remote_copy(
@@ -355,27 +385,25 @@
             send_relayed()
         else:
             spread(functools.partial(send_piece, c))
-        if c >= LAG and not (relay and c - LAG == RELAY):
-            gather_chunk(c - LAG)
+        for at in range(m - 1):
+            if max(sets[at]) == c - LAG:
+                gather(at)
         if relay and c == RELAY_AT:
             pl.when(p != 0)(forward)
     energy = energy + remap_chunk(n - 1)
     e_own[...] = energy
     share_all(e_own, e_az, q, "az", az_count, 0)
     send_last()
-    for c in range(max(n - 1 - LAG, 0), n - 1):
-        gather_chunk(c)
-    if relay:
-        gather_chunk(RELAY)
-    share_wait(e_az, az_count, 0)
-    e_sum[...] = jnp.sum(e_az[...], axis=0)
-    share_all(e_sum, e_rng, p, "rng", rng_count, 1)
-    for i in range(n - 1, n + 3):
+    for at in range(m - 1):
+        if max(sets[at]) > n - 2 - LAG:
+            gather(at)
+    for i in range(m - 1, m + 3):
         table(i).wait()
-    share_wait(e_rng, rng_count, 1)
-    mean = jnp.sum(jnp.sum(e_rng[...], axis=0), axis=(0, 1), keepdims=True) / cells
-    scale = lax.rsqrt(mean + 1e-06)
-    scale_ref[...] = jnp.broadcast_to(scale, scale_ref.shape)
+
+    def energy_on():
+        share_wait(e_az, az_count, 0)
+        e_sum[...] = jnp.sum(e_az[...], axis=0)
+        share_all(e_sum, e_rng, p, "rng", rng_count, 1)
 
     def arrived(s):
         others = recv[n - 1].at[pl.ds(0, az_count - 1), pl.ds(s * step, step)]
@@ -383,15 +411,16 @@
 
     @pl.loop(0, subsets - 1)
     def _(s):
+        pl.when(s == (subsets - 1) // 2)(energy_on)
         arrived(s)
         for k in range(step // 2):
             first = s * step + 2 * k
-            y = y_acc[s * (step // 2) + k] + rows_of(n - 1, first)
+            y = y_acc[s * (step // 2) + k] + rows_of(m - 1, first)
 
             def store(i, lines, value):
                 image_ref[first + i, lines, :] = value
 
-            second_stage(y, scale, twist_ref, b_hi_ref, b_lo_ref, store)
+            second_stage(y, twist_ref, b_hi_ref, b_lo_ref, store)
 
     for c in range(n):
         if relay and c == RELAY:
@@ -402,14 +431,17 @@
     for u in range(len(units)):
         for i in reach:
             pl.when(p >= i + 1)(lambda u=u, i=i: halo(u, i).wait_send())
+    share_wait(e_rng, rng_count, 1)
+    mean = jnp.sum(jnp.sum(e_rng[...], axis=0), axis=(0, 1), keepdims=True) / cells
+    scale_ref[...] = jnp.broadcast_to(lax.rsqrt(mean + 1e-06), scale_ref.shape)
     arrived(subsets - 1)
 
 
-def fused(spec, src, offsets, weights, tables, chunks, counts, step, rng_count, az_count):
+def fused(spec, src, offsets, weights, tables, chunks, sets, counts, step, rng_count, az_count):
     rows, columns = spec.shape[:2]
     blocks = rows // BLOCK
     piece = rows // az_count
-    n = len(chunks)
+    m = len(sets)
     units = units_of(chunks)
     total_groups = columns // 2 * az_count
     cells = float(rows * rng_count * total_groups * GW) * float(total_groups * GW)
@@ -419,24 +451,22 @@
     vmem = pltpu.VMEM
     f32 = jnp.float32
     sizes = [size for _, size in chunks]
-    relays = []
-    if rng_count == 2 and az_count % 4 == 0 and n - 1 - LAG > RELAY_AT and sizes[RELAY] == 1:
-        relays = [vmem((az_count // 4, piece, 1, 1, GW), f32)]
+    relay = [vmem((az_count // 4, piece, 1, 1, GW), f32)] if relays(chunks, rng_count, az_count) else []
     outs = [
         vmem(((piece - step), 2 * total_groups, GW), f32),
         vmem((piece // 2, 2 * total_groups, 2 * GW), f32),
-        vmem((az_count, piece, sizes[-1], 1, GW), f32),
+        vmem((az_count, piece + PAD, sizes[-1], 1, GW), f32),
         vmem(tile, f32),
-    ] + [vmem(t.shape, t.dtype) for t in tables[n - 1:]]
+    ] + [vmem(t.shape, t.dtype) for t in tables[m - 1:]]
     return pl.pallas_call(
-        functools.partial(fused_kernel, rows, blocks, chunks, units, counts, step, cells),
+        functools.partial(fused_kernel, rows, blocks, chunks, sets, units, counts, step, cells),
         out_shape=outs,
         in_specs=[hbm] * (4 + len(tables)),
         out_specs=[pl.BlockSpec(memory_space=vmem)] * len(outs),
-        scratch_shapes=[vmem((rows + sum(counts), width, 1, GW), f32) for _, _, width in units]
+        scratch_shapes=[vmem((rows + sum(counts) + UNUSED, width, 1, GW), f32) for _, _, width in units]
         + [vmem((rows, size, 1, GW), f32) for size in sizes]
-        + [vmem((az_count, piece, size, 1, GW), f32) for size in sizes[:-1]]
-        + [vmem(t.shape, t.dtype) for t in tables[:n - 1]]
+        + [vmem((az_count, piece + PAD, size, 1, GW), f32) for size in sizes[:-1]]
+        + [vmem(t.shape, t.dtype) for t in tables[:m - 1]]
         + [
             pltpu.SMEM(src.shape, src.dtype),
             vmem(offsets.shape, offsets.dtype),
@@ -450,61 +480,63 @@
             dma((len(units),)),
             dma((len(units), len(counts))),
             dma((len(units), len(counts))),
-            dma((n,)),
-            dma((n,)),
+            dma((len(chunks),)),
+            dma((len(chunks),)),
             dma((piece // step,)),
             dma((2,)),
             dma((2,)),
             dma((3,)),
-        ] + relays,
+        ] + relay,
         compiler_params=pltpu.CompilerParams(
             has_side_effects=True, collective_id=0, vmem_limit_bytes=40 * 1024 * 1024),
     )(src, offsets, weights, spec, *tables)
 
 
-def store_kernel(step, band_ref, y_acc, recv, scale_ref, a_ref, twist_ref, b_hi_ref, b_lo_ref, out_ref, end, sem, end_sem):
+def store_kernel(step, band_ref, y_acc, recv, scale_ref, a_ref, twist_ref, b_hi_ref, b_lo_ref, out_ref, scaled, sem, end_sem):
     done = band_ref.shape[0]
-    parts = done // step
-    az_count, piece, sub = recv.shape[:3]
-
-    def copy(i):
+    scale = scale_ref[:1, :1]
+
+    def copy(first, count, at):
+        return pltpu.make_async_copy(scaled.at[pl.ds(first, count)], out_ref.at[pl.ds(first, count)], at)
+
+    @pl.loop(0, done // step)
+    def _(i):
         rows = pl.ds(i * step, step)
-        return pltpu.make_async_copy(band_ref.at[rows], out_ref.at[rows], sem.at[i])
-
-    def copy_end(k):
-        return pltpu.make_async_copy(end.at[pl.ds(2 * k, 2)], out_ref.at[pl.ds(done + 2 * k, 2)], end_sem.at[k])
-
-    for i in range(parts):
-        copy(i).start()
+        scaled[rows] = band_ref[rows] * scale
+        copy(i * step, step, sem.at[i]).start()
 
     @pl.loop(0, step // 2)
     def _(k):
         first = done + 2 * k
-        y = y_acc[first // 2] + first_stage(recv, a_ref, sub, piece, az_count, first, piece)
+        y = y_acc[first // 2] + first_stage([recv], a_ref, first)
 
         def store(i, lines, value):
-            end[2 * k + i, lines, :] = value
-
-        second_stage(y, scale_ref[:1, :1], twist_ref, b_hi_ref, b_lo_ref, store)
-        copy_end(k).start()
-
-    for i in range(parts):
-        copy(i).wait()
-    for k in range(step // 2):
-        copy_end(k).wait()
+            scaled[first + i, lines, :] = value * scale
+
+        second_stage(y, twist_ref, b_hi_ref, b_lo_ref, store)
+        copy(first, 2, end_sem.at[k]).start()
+
+    @pl.loop(0, done // step)
+    def _(i):
+        copy(i * step, step, sem.at[i]).wait()
+
+    @pl.loop(0, step // 2)
+    def _(k):
+        copy(done + 2 * k, 2, end_sem.at[k]).wait()
 
 
 def store(step, rows, band, *rest):
     parts = rows // step
     vmem = pltpu.VMEM
+    shape = (rows,) + band.shape[1:]
     return pl.pallas_call(
         functools.partial(store_kernel, step),
-        out_shape=jax.ShapeDtypeStruct((rows,) + band.shape[1:], band.dtype),
+        out_shape=jax.ShapeDtypeStruct(shape, band.dtype),
         in_specs=[pl.BlockSpec(memory_space=vmem)] * (1 + len(rest)),
         out_specs=pl.BlockSpec(memory_space=pl.ANY),
-        scratch_shapes=[vmem((step,) + band.shape[1:], band.dtype), pltpu.SemaphoreType.DMA((parts - 1,)),
+        scratch_shapes=[vmem(shape, band.dtype), pltpu.SemaphoreType.DMA((parts - 1,)),
                         pltpu.SemaphoreType.DMA((step // 2,))],
-        compiler_params=pltpu.CompilerParams(vmem_limit_bytes=12 * 1024 * 1024),
+        compiler_params=pltpu.CompilerParams(vmem_limit_bytes=20 * 1024 * 1024),
     )(band, *rest)
 
 
@@ -513,7 +545,7 @@
     halo = min(rows_dev - BLOCK + SHIFT_B * BLOCK, total - 2 * BLOCK) + WINDOW - rows_dev
     counts = []
     while halo > 0:
-        counts.append(min(halo, rows_dev))
+        counts.append(min(halo, rows_dev) if halo > rows_dev else halo - UNUSED)
         halo -= rows_dev
     return counts
 
@@ -527,11 +559,12 @@
     rows_after = rows_dev // az_count
     total_len = columns * az_count
     chunks = plan(groups)
-    tables = [jnp.asarray(t) for t in dft_tables(az_count, groups, chunks)]
+    sets = gather_sets(chunks, relays(chunks, rng_count, az_count))
+    tables = [jnp.asarray(t) for t in dft_tables(az_count, groups, chunks, sets)]
     spec = spectrum.reshape(rows_dev, 2, groups, GW).transpose(0, 2, 1, 3).reshape(rows_dev, 2 * groups, 1, GW)
     counts = halo_counts(rows_dev, rng_count)
     step = min(STEP, rows_after // 2)
-    held = fused(spec, src_block.T, offsets, tap_weights, tables, chunks, counts, step, rng_count, az_count)
+    held = fused(spec, src_block.T, offsets, tap_weights, tables, chunks, sets, counts, step, rng_count, az_count)
     image = store(step, rows_after, *held)
     return (
         image.reshape(rows_after, total_len // GW, 2, GW)

time: 203 us -> 197 us (0.970)
  Pallas kernels: 202 us -> 197 us
    pallas_call x1, Pallas kernels: 199 us -> 194 us  [fused(): pl.pallas_call(functools.partial(fused_kernel, rows, blocks, chunks, sets...]
where the time goes in v4:
time: 197 us
  Pallas kernels  197 us (100%)
    pallas_call x1, Pallas kernels, fused(): pl.pallas_call(functools.partial(fused_kernel, rows, blocks, chunks, sets...  194 us

profile of v4, /device:TPU:0, one launch (start us, length us, event | category | flops | bytes accessed | tf_op | source)
XLA Modules:
  0.0 197.2 jit_solution(5442007479923484068)
XLA Ops:
  0.0 193.7 %shard_map.145 = (f32[28,512,128]{2,1,0:T(8,128)S(1)}, f32[16,512,256]{2,1,0:T(8,128)S(1)}, f32[16,33,6,1,128]{4,3,2,1,0:T(1,128)S(1)}, f32[8,128]{1,0:T(8,128)S...) custom-call(s32[4,16]{1,0:T(4,128)} %bitcast.12, ...), custom_call_target="tpu_custom_call" | custom-call | tf_op jit(solution)/shard_map/pallas_call | solution.py:461
  193.7 3.5 %shard_map.146 = f32[32,512,128]{2,1,0:T(8,128)} custom-call(f32[28,512,128]{2,1,0:T(8,128)S(1)} %get-tuple-element.13.band_ref, f32[16,512,256]{2,1,0:T(8,128)S(1)} %get-tuple-element.14.y_acc, f32[16,33,6,1,128]{4,3,2,1,0:T(1,128)S(1)} %get-tuple-element.15.recv, f32[8,128]{1,0:T(8,128)S(1)} %get-tuple-element.16.scale_ref, ...), custom_call_target="tpu_custom_call" | custom-call | tf_op jit(solution)/shard_map/pallas_call | solution.py:532

commit v5 on v4

--- a/solution.py
+++ b/solution.py
@@ -14,7 +14,7 @@
 SHIFT_B = 5
 WINDOW = 144
 UNUSED = WINDOW - (BLOCK - 1 + TAPS)
-LAG = 2
+LAG = 3
 RELAY = 7
 RELAY_AT = 10
 STEP = 4
@@ -334,16 +334,35 @@
         keep(0)
         return energy
 
+    def send_rows(r, peer):
+        c = n - 1
+        pltpu.make_async_remote_copy(
+            src_ref=stage[c].at[pl.ds(peer * piece + r * step, step)],
+            dst_ref=recv[c].at[q, pl.ds(r * step, step)],
+            send_sem=part_send.at[c], recv_sem=last_recv.at[r],
+            device_id={"az": peer}, device_id_type=MESH).start()
+
     def send_last():
-        c = n - 1
-
-        @pl.loop(0, subsets)
+        @pl.loop(0, subsets - 2)
         def _(r):
-            spread(lambda peer: pltpu.make_async_remote_copy(
-                src_ref=stage[c].at[pl.ds(peer * piece + r * step, step)],
-                dst_ref=recv[c].at[q, pl.ds(r * step, step)],
-                send_sem=part_send.at[c], recv_sem=last_recv.at[r],
-                device_id={"az": peer}, device_id_type=MESH).start())
+            spread(functools.partial(send_rows, r))
+
+        quarter = max(half // 2, 1)
+        turn = jnp.where(side == 0, place // quarter, 0)
+
+        @pl.loop(0, half // quarter)
+        def _(h):
+            @pl.loop(subsets - 2, subsets)
+            def _(r):
+                @pl.loop(0, quarter)
+                def _(j):
+                    send_rows(r, (1 - side) * half + (h + turn) % (half // quarter) * quarter + (place + j) % quarter)
+
+        @pl.loop(subsets - 2, subsets)
+        def _(r):
+            @pl.loop(1, half)
+            def _(j):
+                send_rows(r, side * half + (place + j) % half)
 
     def rows_of(at, row):
         return first_stage([recv[c] for c in sets[at]], a_refs[at], row)

time: 197 us -> 196 us (level)
  no operation moved by 1% of the time
where the time goes in v5:
time: 196 us
  Pallas kernels  196 us (100%)
    pallas_call x1, Pallas kernels, fused(): pl.pallas_call(functools.partial(fused_kernel, rows, blocks, chunks, sets...  193 us

profile of v5, /device:TPU:0, one launch (start us, length us, event | category | flops | bytes accessed | tf_op | source)
XLA Modules:
  0.0 196.3 jit_solution(17620626531147712560)
XLA Ops:
  0.0 192.8 %shard_map.145 = (f32[28,512,128]{2,1,0:T(8,128)S(1)}, f32[16,512,256]{2,1,0:T(8,128)S(1)}, f32[16,33,6,1,128]{4,3,2,1,0:T(1,128)S(1)}, f32[8,128]{1,0:T(8,128)S...) custom-call(s32[4,16]{1,0:T(4,128)} %bitcast.12, ...), custom_call_target="tpu_custom_call" | custom-call | tf_op jit(solution)/shard_map/pallas_call | solution.py:480
  192.8 3.5 %shard_map.146 = f32[32,512,128]{2,1,0:T(8,128)} custom-call(f32[28,512,128]{2,1,0:T(8,128)S(1)} %get-tuple-element.13.band_ref, f32[16,512,256]{2,1,0:T(8,128)S(1)} %get-tuple-element.14.y_acc, f32[16,33,6,1,128]{4,3,2,1,0:T(1,128)S(1)} %get-tuple-element.15.recv, f32[8,128]{1,0:T(8,128)S(1)} %get-tuple-element.16.scale_ref, ...), custom_call_target="tpu_custom_call" | custom-call | tf_op jit(solution)/shard_map/pallas_call | solution.py:551

commit v6 on v5

--- a/solution.py
+++ b/solution.py
@@ -277,7 +277,7 @@
     def hand_over(peer):
         pltpu.make_async_remote_copy(
             src_ref=stage[RELAY].at[pl.ds(peer * piece, piece)],
-            dst_ref=relay[0].at[peer % half // 2],
+            dst_ref=relay[0].at[peer % half],
             send_sem=relay_sem.at[0], recv_sem=relay_sem.at[1],
             device_id={"rng": 1 - p}, device_id_type=MESH).start()
 
@@ -285,7 +285,8 @@
         @pl.loop(0, half)
         def _(j):
             peer = (1 - side) * half + (place + j) % half
-            via = (p == 0) & (peer % 2 == 0)
+            slot = peer % half
+            via = (p == 0) & ((slot < half // 2) | (slot == half - 1))
             pl.when(via)(lambda: hand_over(peer))
             pl.when(jnp.logical_not(via))(lambda: send_piece(RELAY, peer))
 
@@ -294,26 +295,30 @@
             send_piece(RELAY, side * half + (place + j) % half)
 
     def forward():
-        pltpu.make_async_copy(relay[0], relay[0], relay_sem.at[1]).wait()
-
-        @pl.loop(0, half // 2)
-        def _(i):
-            pltpu.make_async_remote_copy(
-                src_ref=relay[0].at[i],
+        sent = relay[0].at[pl.ds(0, (half // 2 + 1))]
+        pltpu.make_async_copy(sent, sent, relay_sem.at[1]).wait()
+
+        @pl.loop(0, half)
+        def _(slot):
+            copy = pltpu.make_async_remote_copy(
+                src_ref=relay[0].at[slot],
                 dst_ref=recv[RELAY].at[q, pl.ds(0, piece)],
                 send_sem=relay_sem.at[2], recv_sem=part_recv.at[RELAY],
-                device_id={"rng": 1 - p, "az": (1 - side) * half + 2 * i}, device_id_type=MESH).start()
+                device_id={"rng": 1 - p, "az": (1 - side) * half + slot}, device_id_type=MESH)
+            pl.when((slot < half // 2) | (slot == half - 1))(copy.start)
 
     def relay_done():
         def handed():
-            sent = stage[RELAY].at[pl.ds(0, rows - piece - half // 2 * piece)]
+            sent = stage[RELAY].at[pl.ds(0, rows - piece - (half // 2 + 1) * piece)]
             pltpu.make_async_copy(sent, sent, part_send.at[RELAY]).wait()
-            pltpu.make_async_copy(relay[0], relay[0], relay_sem.at[0]).wait()
+            via = relay[0].at[pl.ds(0, (half // 2 + 1))]
+            pltpu.make_async_copy(via, via, relay_sem.at[0]).wait()
 
         def forwarded():
             sent = stage[RELAY].at[pl.ds(0, rows - piece)]
             pltpu.make_async_copy(sent, sent, part_send.at[RELAY]).wait()
-            pltpu.make_async_copy(relay[0], relay[0], relay_sem.at[2]).wait()
+            via = relay[0].at[pl.ds(0, (half // 2 + 1))]
+            pltpu.make_async_copy(via, via, relay_sem.at[2]).wait()
 
         pl.when(p == 0)(handed)
         pl.when(p != 0)(forwarded)
@@ -470,7 +475,7 @@
     vmem = pltpu.VMEM
     f32 = jnp.float32
     sizes = [size for _, size in chunks]
-    relay = [vmem((az_count // 4, piece, 1, 1, GW), f32)] if relays(chunks, rng_count, az_count) else []
+    relay = [vmem((az_count // 2, piece, 1, 1, GW), f32)] if relays(chunks, rng_count, az_count) else []
     outs = [
         vmem(((piece - step), 2 * total_groups, GW), f32),
         vmem((piece // 2, 2 * total_groups, 2 * GW), f32),
@@ -524,12 +529,11 @@
         scaled[rows] = band_ref[rows] * scale
         copy(i * step, step, sem.at[i]).start()
 
-    @pl.loop(0, step // 2)
-    def _(k):
+    for k in range(step // 2):
         first = done + 2 * k
         y = y_acc[first // 2] + first_stage([recv], a_ref, first)
 
-        def store(i, lines, value):
+        def store(i, lines, value, first=first):
             scaled[first + i, lines, :] = value * scale
 
         second_stage(y, twist_ref, b_hi_ref, b_lo_ref, store)

time: 196 us -> 196 us (level)
  no operation moved by 1% of the time
where the time goes in v6:
time: 196 us
  Pallas kernels  196 us (100%)
    pallas_call x1, Pallas kernels, fused(): pl.pallas_call(functools.partial(fused_kernel, rows, blocks, chunks, sets...  192 us

profile of v6, /device:TPU:0, one launch (start us, length us, event | category | flops | bytes accessed | tf_op | source)
XLA Modules:
  0.0 195.7 jit_solution(9046886242046067260)
XLA Ops:
  0.0 192.2 %shard_map.145 = (f32[28,512,128]{2,1,0:T(8,128)S(1)}, f32[16,512,256]{2,1,0:T(8,128)S(1)}, f32[16,33,6,1,128]{4,3,2,1,0:T(1,128)S(1)}, f32[8,128]{1,0:T(8,128)S...) custom-call(s32[4,16]{1,0:T(4,128)} %bitcast.12, ...), custom_call_target="tpu_custom_call" | custom-call | tf_op jit(solution)/shard_map/pallas_call | solution.py:485
  192.2 3.5 %shard_map.146 = f32[32,512,128]{2,1,0:T(8,128)} custom-call(f32[28,512,128]{2,1,0:T(8,128)S(1)} %get-tuple-element.13.band_ref, f32[16,512,256]{2,1,0:T(8,128)S(1)} %get-tuple-element.14.y_acc, f32[16,33,6,1,128]{4,3,2,1,0:T(1,128)S(1)} %get-tuple-element.15.recv, f32[8,128]{1,0:T(8,128)S(1)} %get-tuple-element.16.scale_ref, ...), custom_call_target="tpu_custom_call" | custom-call | tf_op jit(solution)/shard_map/pallas_call | solution.py:555
